TPU v7x, 8 devices: a whole 2x2x1 slice. The times are simulated.
8 devices in a mesh: layer: 1 (over z), tp: 2 (over y), fsdp: 4 (over x, core).
Axes of the slice: x: 2, y: 2, z: 1, core: 2. Of those that a mesh axis runs over, the one named last changes fastest.
Arguments:
- wq_weight: float32 [1024, 1024], P(('layer', 'fsdp'), 'tp')
- wq_moment: float32 [1024, 1024], P(('layer', 'fsdp'), 'tp')
- wq_grad: bfloat16 [1024, 1024], P(('layer', 'fsdp'), 'tp')
- wq_factor: float32 [1024, 64], P(('layer', 'tp'))
- wk_weight: float32 [1024, 512], P(('layer', 'fsdp'), 'tp')
- wk_moment: float32 [1024, 512], P(('layer', 'fsdp'), 'tp')
- wk_grad: bfloat16 [1024, 512], P(('layer', 'fsdp'), 'tp')
- wk_factor: float32 [512, 32], P(('layer', 'tp'))
- wv_weight: float32 [1024, 512], P(('layer', 'fsdp'), 'tp')
- wv_moment: float32 [1024, 512], P(('layer', 'fsdp'), 'tp')
- wv_grad: bfloat16 [1024, 512], P(('layer', 'fsdp'), 'tp')
- wv_factor: float32 [512, 32], P(('layer', 'tp'))
- wo_weight: float32 [1024, 1024], P(('layer', 'fsdp'), 'tp')
- wo_moment: float32 [1024, 1024], P(('layer', 'fsdp'), 'tp')
- wo_grad: bfloat16 [1024, 1024], P(('layer', 'fsdp'), 'tp')
- wo_factor: float32 [1024, 64], P(('layer', 'tp'))
- gate_weight: float32 [32, 1024, 512], P('layer', 'fsdp', 'tp')
- gate_moment: float32 [32, 1024, 512], P('layer', 'fsdp', 'tp')
- gate_grad: bfloat16 [32, 1024, 512], P('layer', 'fsdp', 'tp')
- gate_factor: float32 [32, 512, 32], P('layer', 'tp')
- up_weight: float32 [32, 1024, 512], P('layer', 'fsdp', 'tp')
- up_moment: float32 [32, 1024, 512], P('layer', 'fsdp', 'tp')
- up_grad: bfloat16 [32, 1024, 512], P('layer', 'fsdp', 'tp')
- up_factor: float32 [32, 512, 32], P('layer', 'tp')
- down_weight: float32 [32, 512, 1024], P('layer', 'fsdp', 'tp')
- down_moment: float32 [32, 512, 1024], P('layer', 'fsdp', 'tp')
- down_grad: bfloat16 [32, 512, 1024], P('layer', 'fsdp', 'tp')
- down_factor: float32 [32, 512, 32], P('layer', 'fsdp')
Outputs:
- output 1: float32 [1024, 1024], P(('layer', 'fsdp'), 'tp')
- output 2: float32 [1024, 1024], P(('layer', 'fsdp'), 'tp')
- output 3: float32 [1024, 64], P(('layer', 'tp'))
- output 4: float32 [1024, 512], P(('layer', 'fsdp'), 'tp')
- output 5: float32 [1024, 512], P(('layer', 'fsdp'), 'tp')
- output 6: float32 [512, 32], P(('layer', 'tp'))
- output 7: float32 [1024, 512], P(('layer', 'fsdp'), 'tp')
- output 8: float32 [1024, 512], P(('layer', 'fsdp'), 'tp')
- output 9: float32 [512, 32], P(('layer', 'tp'))
- output 10: float32 [1024, 1024], P(('layer', 'fsdp'), 'tp')
- output 11: float32 [1024, 1024], P(('layer', 'fsdp'), 'tp')
- output 12: float32 [1024, 64], P(('layer', 'tp'))
- output 13: float32 [32, 1024, 512], P('layer', 'fsdp', 'tp')
- output 14: float32 [32, 1024, 512], P('layer', 'fsdp', 'tp')
- output 15: float32 [32, 512, 32], P('layer', 'tp')
- output 16: float32 [32, 1024, 512], P('layer', 'fsdp', 'tp')
- output 17: float32 [32, 1024, 512], P('layer', 'fsdp', 'tp')
- output 18: float32 [32, 512, 32], P('layer', 'tp')
- output 19: float32 [32, 512, 1024], P('layer', 'fsdp', 'tp')
- output 20: float32 [32, 512, 1024], P('layer', 'fsdp', 'tp')
- output 21: float32 [32, 512, 32], P('layer', 'fsdp')
All inputs are finite; a program needn't handle non-finite values.
Results may differ from a plain program's by a relative error of at most 0.001.
Values are sent between devices in bfloat16 or wider.
A program may use at most 1 GiB of HBM per device.

v0:
```python
import math
import jax
import jax.numpy as jnp
from jax import lax
from jax.sharding import PartitionSpec as P

MOMENTUM = 0.9
LEARN_RATE = 0.3
FULL_PREC = lax.Precision.HIGHEST
KEEP_FORMS = ('bmn,bnr->bmr', 'bmn,bmr->bnr', 'bmr,bnr->bmn')
FLIP_FORMS = ('bnm,bnr->bmr', 'bnm,bmr->bnr', 'bmr,bnr->bnm')


def mat_mul(form, left_op, right_op):
    return jnp.einsum(form, left_op, right_op, preferred_element_type=jnp.float32, precision=FULL_PREC)


def dion_local(weight, moment, gradient, factor, forms, long_axis, short_axis, long_size, short_size):
    mom_grad = moment + gradient.astype(jnp.float32)
    p_tilde = lax.psum(mat_mul(forms[0], mom_grad, factor), short_axis)
    gram_mat = lax.psum(mat_mul('bmr,bms->brs', p_tilde, p_tilde), long_axis)
    chol_low = jnp.linalg.cholesky(gram_mat)
    p_orth = lax.linalg.triangular_solve(chol_low, p_tilde, left_side=False, lower=True, transpose_a=True)
    r_new = lax.psum(mat_mul(forms[1], mom_grad, p_orth), long_axis)
    moment_new = mom_grad - (1.0 - MOMENTUM) * mat_mul(forms[2], p_orth, r_new)
    col_sq = lax.psum(jnp.sum(r_new * r_new, axis=1, keepdims=True), short_axis)
    factor_new = r_new / jnp.sqrt(col_sq)
    step_scale = LEARN_RATE * math.sqrt(p_tilde.shape[1] * long_size / (factor.shape[1] * short_size))
    weight_new = weight - step_scale * mat_mul(forms[2], p_orth, factor_new)
    return weight_new, moment_new, factor_new


def solution(mesh):
    fsdp_size = mesh.shape['fsdp']
    tp_size = mesh.shape['tp']
    dense_w = P(('layer', 'fsdp'), 'tp')
    dense_f = P(('layer', 'tp'), None)
    stack_w = P('layer', 'fsdp', 'tp')
    stack_f = P('layer', 'tp', None)
    down_f = P('layer', 'fsdp', None)
    in_specs = (dense_w, dense_w, dense_w, dense_f) * 4 + (stack_w, stack_w, stack_w, stack_f) * 2 + (stack_w, stack_w, stack_w, down_f)
    out_specs = (dense_w, dense_w, dense_f) * 4 + (stack_w, stack_w, stack_f) * 2 + (stack_w, stack_w, down_f)

    def local_step(*blocks):
        results = []
        for mat_idx in range(4):
            group_in = [local_arr[None] for local_arr in blocks[4 * mat_idx:4 * mat_idx + 4]]
            updated = dion_local(group_in[0], group_in[1], group_in[2], group_in[3], KEEP_FORMS, 'fsdp', 'tp', fsdp_size, tp_size)
            results.extend([item_out[0] for item_out in updated])
        for mat_idx in (4, 5):
            group_in = blocks[4 * mat_idx:4 * mat_idx + 4]
            results.extend(dion_local(group_in[0], group_in[1], group_in[2], group_in[3], KEEP_FORMS, 'fsdp', 'tp', fsdp_size, tp_size))
        group_in = blocks[24:28]
        results.extend(dion_local(group_in[0], group_in[1], group_in[2], group_in[3], FLIP_FORMS, 'tp', 'fsdp', tp_size, fsdp_size))
        return tuple(results)

    return jax.shard_map(local_step, mesh=mesh, in_specs=in_specs, out_specs=out_specs, check_vma=False)
```

profile of v0, /device:TPU:0, one launch (start us, length us, event | category | flops | bytes accessed | tf_op | source)
XLA Modules:
  0.0 775.5 jit_solution(4080190527870948565)
XLA Ops:
  11.5 13.8 %fusion.1 = f32[32,256,32]{1,2,0:T(8,128)} fusion(f32[32,256,32]{1,2,0:T(8,128)S(1)} %copy-done, f32[32,256,256]{2,1,0:T(8,128)} %param.54, bf16[32,256,256]{2,1,0:T(8,128)(2,1)} %param.55), kind=kOutput, calls=%fused_computation.10 | convolution fusion | flops 809500672 | bytes 14680064 | tf_op jit(solution)/shard_map/bmn,bnr->bmr/dot_general | solution.py:15
  25.4 18.0 %fusion.3 = f32[32,256,32]{1,2,0:T(8,128)} fusion(f32[32,256,32]{1,2,0:T(8,128)S(1)} %copy-done.26, f32[32,256,256]{2,1,0:T(8,128)S(1)} %copy-done.2, bf16[32,256,256]{2,1,0:T(8,128)(2,1)S(1)} %copy-done.3), kind=kOutput, calls=%fused_computation.12 | convolution fusion | flops 809500672 | bytes 14680064 | tf_op jit(solution)/shard_map/bmn,bnr->bmr/dot_general | solution.py:15
  57.0 13.8 %all-reduce.1 = (f32[1,32,32]{1,2,0:T(8,128)S(1)}, f32[1,32,32]{1,2,0:T(8,128)S(1)}) all-reduce(f32[1,32,32]{1,2,0:T(8,128)S(1)} %convolution_bitcast_fusion.17, f32[1,32,32]{1,2,0:T(8,128)S(1)} %convolution_bitcast_fusion.16), channel_id=1, replica_groups=mesh['layer'=1,'tp'=2,'fsdp'=4] {'fsdp'}, use_global_device_ids=true, to_apply=%region_8.0 | all-reduce | flops 2048 | bytes 16384 | tf_op jit(solution)/shard_map/psum | solution.py:21
  74.6 29.0 %all-reduce.28.cloned.1.call-done = (f32[32,256,32]{1,2,0:T(8,128)}, f32[32,256,32]{1,2,0:T(8,128)}) async-done(((f32[32,256,32]{1,2,0:T(8,128)}, f32[32,256,32]{1,2,0:T(8,128)}), (f32[32,256,32]{1,2,0:T(8,128)}, f32[32,256,32]{1,2,0:T(8,128)})) %all-reduce.28.cloned.1.call-update) | async-done | bytes 2097168 | tf_op jit(solution)/shard_map/psum | solution.py:20
  122.6 50.8 %all-reduce.22.cloned.1.call-done = (f32[32,512,32]{1,2,0:T(8,128)}, f32[32,32,32]{1,2,0:T(8,128)}, f32[32,32,32]{1,2,0:T(8,128)}) async-done(((f32[32,512,32]{1,2,0:T(8,128)}, f32[32,32,32]{1,2,0:T(8,128)}, f32[32,32,32]{1,2,0:T(8,128)}), (f32[32,512,32]{1,2,0:T(8,128)}, f32[32,32,32]{1,2,0:T(8,128)}, f32[32,32,32]{1,2,0:T(8,128)})) %all-reduce.22.cloned.1.call-update) | async-done | bytes 2359312 | tf_op jit(solution)/shard_map/psum | solution.py:20
  182.8 93.8 %custom-call.37 = f32[32,32,32]{2,1,0:T(8,128)S(1)} custom-call(f32[32,32,32]{2,1,0:T(8,128)S(1)} %get-tuple-element.61), custom_call_target="Cholesky" | custom-call | tf_op jit(solution)/shard_map/jit(cholesky)/cholesky | solution.py:22
  276.9 93.8 %custom-call.39 = f32[32,32,32]{2,1,0:T(8,128)S(1)} custom-call(f32[32,32,32]{2,1,0:T(8,128)S(1)} %get-tuple-element.60), custom_call_target="Cholesky" | custom-call | tf_op jit(solution)/shard_map/jit(cholesky)/cholesky | solution.py:22
  373.4 93.8 %custom-call.41 = f32[32,32,32]{2,1,0:T(8,128)S(1)} custom-call(f32[32,32,32]{2,1,0:T(8,128)S(1)} %fusion.14), custom_call_target="Cholesky" | custom-call | tf_op jit(solution)/shard_map/jit(cholesky)/cholesky | solution.py:22
  469.1 12.5 %custom-call.21 = f32[32,1,32,32]{0,2,3,1:T(8,128)S(1)} custom-call(f32[32,1,32,32]{0,3,2,1:T(8,128)S(1)} %get-tuple-element.58), custom_call_target="InvertDiagBlocksLowerTriangular" | custom-call | tf_op jit(solution)/shard_map/triangular_solve | solution.py:23
  485.6 12.6 %fusion.4 = f32[32,128,32]{1,2,0:T(8,128)} fusion(f32[32,512,32]{1,2,0:T(8,128)S(1)} %fusion.45, f32[32,128,512]{2,1,0:T(8,128)} %param.62, bf16[32,128,512]{2,1,0:T(8,128)(2,1)} %param.63), kind=kOutput, calls=%fused_computation.13 | convolution fusion | flops 809500672 | bytes 15204352 | tf_op jit(solution)/shard_map/bnm,bmr->bnr/dot_general | solution.py:15
  498.2 13.8 %custom-call.38 = f32[32,1,32,32]{0,2,3,1:T(8,128)S(1)} custom-call(f32[32,1,32,32]{0,3,2,1:T(8,128)} %get-tuple-element.59), custom_call_target="InvertDiagBlocksLowerTriangular" | custom-call | tf_op jit(solution)/shard_map/triangular_solve/custom-call.5 | solution.py:23
  515.8 11.6 %fusion = f32[32,256,32]{1,2,0:T(8,128)} fusion(f32[32,256,32]{1,2,0:T(8,128)S(1)} %convolution_bitcast_fusion.1, f32[32,256,256]{2,1,0:T(8,128)} %param.54, bf16[32,256,256]{2,1,0:T(8,128)(2,1)} %param.55), kind=kOutput, calls=%fused_computation.9 | convolution fusion | flops 809500672 | bytes 14680064 | tf_op jit(solution)/shard_map/bmn,bmr->bnr/dot_general | solution.py:15
  527.4 14.2 %custom-call.40 = f32[32,1,32,32]{0,2,3,1:T(8,128)} custom-call(f32[32,1,32,32]{0,3,2,1:T(8,128)} %get-tuple-element.57), custom_call_target="InvertDiagBlocksLowerTriangular" | custom-call | tf_op jit(solution)/shard_map/triangular_solve/custom-call.5 | solution.py:23
  547.3 11.5 %fusion.2 = f32[32,256,32]{1,2,0:T(8,128)} fusion(f32[32,256,32]{1,2,0:T(8,128)} %convolution_bitcast_fusion, f32[32,256,256]{2,1,0:T(8,128)} %param.58, bf16[32,256,256]{2,1,0:T(8,128)(2,1)} %param.59), kind=kOutput, calls=%fused_computation.11 | convolution fusion | flops 809500672 | bytes 14680064 | tf_op jit(solution)/shard_map/bmn,bmr->bnr/dot_general | solution.py:15
  558.9 14.4 %all-reduce.26.cloned.1.call-done = (f32[1,256,64]{1,2,0:T(8,128)}, f32[1,256,64]{1,2,0:T(8,128)}, f32[32,128,32]{1,2,0:T(8,128)}) async-done(((f32[1,256,64]{1,2,0:T(8,128)}, f32[1,256,64]{1,2,0:T(8,128)}, f32[32,128,32]{1,2,0:T(8,128)}), (f32[1,256,64]{1,2,0:T(8,128)}, f32[1,256,64]{1,2,0:T(8,128)}, f32[32,128,32]{1,2,0:T(8,128)})) %all-reduce.26.cloned.1.call-update) | async-done | bytes 655376 | tf_op jit(solution)/shard_map/psum | solution.py:20
  578.9 12.8 %multiply_subtract_fusion = f32[32,128,512]{2,1,0:T(8,128)} fusion(f32[32,128,32]{1,2,0:T(8,128)} %get-tuple-element.54, f32[32,512,32]{1,2,0:T(8,128)S(1)} %fusion.45, f32[32,128,512]{2,1,0:T(8,128)} %param.62, bf16[32,128,512]{2,1,0:T(8,128)(2,1)} %param.63), kind=kOutput, calls=%fused_computation | convolution fusion | flops 813694976 | bytes 23592960 | tf_op jit(solution)/shard_map/bmr,bnr->bnm/dot_general | solution.py:15
  591.6 13.8 %all-reduce.18.cloned.1.call-done = (f32[1,64,64]{1,2,0:T(8,128)}, f32[1,256,32]{1,2,0:T(8,128)}, f32[1,256,32]{1,2,0:T(8,128)}, f32[1,64,64]{1,2,0:T(8,128)}, f32[32,1,32]{2,0,1:T(8,128)}) async-done(((f32[1,64,64]{1,2,0:T(8,128)}, f32[1,256,32]{1,2,0:T(8,128)}, f32[1,256,32]{1,2,0:T(8,128)}, f32[1,64,64]{1,2,0:T(8,128)}, f32[32,1,32]{2,0,1:T(8,128)}), (f32[1,64,64]{1,2,0:T(8,128)}, ...) | async-done | bytes 102416 | tf_op jit(solution)/shard_map/psum | solution.py:21
  649.2 11.7 %multiply_subtract_fusion.1 = f32[32,128,512]{2,1,0:T(8,128)} fusion(f32[32,128,512]{2,1,0:T(8,128)} %param.61, f32[32,128,32]{1,2,0:T(8,128)S(1)} %broadcast_divide_fusion.2, f32[32,512,32]{1,2,0:T(8,128)S(1)} %fusion.45), kind=kOutput, calls=%fused_computation.1 | convolution fusion | flops 809500672 | bytes 19398656 | tf_op jit(solution)/shard_map/bmr,bnr->bnm/dot_general | solution.py:15
  660.9 35.7 %all-reduce.20.cloned.1.call-done = (f32[1,512,64]{1,2,0:T(8,128)}, f32[1,512,64]{1,2,0:T(8,128)}, f32[32,256,32]{1,2,0:T(8,128)}, f32[32,256,32]{1,2,0:T(8,128)}) async-done(((f32[1,512,64]{1,2,0:T(8,128)}, f32[1,512,64]{1,2,0:T(8,128)}, f32[32,256,32]{1,2,0:T(8,128)}, f32[32,256,32]{1,2,0:T(8,128)}), (f32[1,512,64]{1,2,0:T(8,128)}, f32[1,512,64]{1,2,0:T(8,128)}, f32[32,256,32]{1,2,0:T(8,128)}, ...) | async-done | bytes 2359312 | tf_op jit(solution)/shard_map/psum | solution.py:24
  698.0 13.2 %multiply_subtract_fusion.2 = f32[32,256,256]{2,1,0:T(8,128)} fusion(f32[32,256,32]{1,2,0:T(8,128)} %convolution_bitcast_fusion, f32[32,256,32]{1,2,0:T(8,128)} %get-tuple-element.40, f32[32,256,256]{2,1,0:T(8,128)} %param.58, bf16[32,256,256]{2,1,0:T(8,128)(2,1)} %param.59), kind=kOutput, calls=%fused_computation.3 | convolution fusion | flops 813694976 | bytes 23068672 | tf_op jit(solution)/shard_map/bmr,bnr->bmn/dot_general | solution.py:15
  712.1 12.4 %multiply_subtract_fusion.4 = f32[32,256,256]{2,1,0:T(8,128)} fusion(f32[32,256,32]{1,2,0:T(8,128)S(1)} %convolution_bitcast_fusion.1, f32[32,256,32]{1,2,0:T(8,128)S(1)} %copy-done.8, f32[32,256,256]{2,1,0:T(8,128)} %param.54, bf16[32,256,256]{2,1,0:T(8,128)(2,1)S(1)} %copy-done.4), kind=kOutput, calls=%fused_computation.6 | convolution fusion | flops 813694976 | bytes 23068672 | tf_op jit(solution)/shard_map/bmr,bnr->bmn/dot_general | solution.py:15
  727.7 9.2 %all-reduce.4 = (f32[1,1,64]{2,1,0:T(1,128)S(1)}, f32[1,1,32]{2,1,0:T(1,128)S(1)}, f32[1,1,32]{2,1,0:T(1,128)S(1)}, f32[1,1,64]{2,1,0:T(1,128)S(1)}, f32[32,1,32]{2,0,1:T(8,128)S(1)}, /*index=5*/f32[32,1,32]{2,0,1:T(8,128)S(1)}) all-reduce(f32[1,1,64]{2,1,0:T(1,128)S(1)} %bitcast.235, ...), channel_id=1, replica_groups=mesh['layer'=1,'tp'=2,'fsdp'=4] {'tp'}, use_global_device_ids=true, to_apply=%region_6.9 | all-reduce | flops 2240 | bytes 17920 | tf_op jit(solution)/shard_map/psum | solution.py:26
  741.6 11.6 %multiply_subtract_fusion.3 = f32[32,256,256]{2,1,0:T(8,128)} fusion(f32[32,256,256]{2,1,0:T(8,128)} %param.57, f32[32,256,32]{1,2,0:T(8,128)S(1)} %copy-done.7, f32[32,256,32]{1,2,0:T(8,128)S(1)} %broadcast_divide_fusion), kind=kOutput, calls=%fused_computation.4 | convolution fusion | flops 809500672 | bytes 18874368 | tf_op jit(solution)/shard_map/bmr,bnr->bmn/dot_general | solution.py:15
  753.4 9.7 %multiply_subtract_fusion.5 = f32[32,256,256]{2,1,0:T(8,128)} fusion(f32[32,256,256]{2,1,0:T(8,128)S(1)} %bitcast.225, f32[32,256,32]{1,2,0:T(8,128)S(1)} %copy-done.6, f32[32,256,32]{1,2,0:T(8,128)S(1)} %broadcast_divide_fusion.1), kind=kOutput, calls=%fused_computation.7 | convolution fusion | flops 809500672 | bytes 18874368 | tf_op jit(solution)/shard_map/bmr,bnr->bmn/dot_general | solution.py:15
  (206 shorter events, 132.7 us)
Async XLA Ops:
  7.2 47.7 %all-reduce.24.cloned.1.call-start = ((), (), s32[]{:S(2)}) async-start(), calls=%async_computation.4 | async-start | bytes 131072 | tf_op jit(solution)/shard_map/psum | solution.py:20
  11.4 92.2 %all-reduce.28.cloned.1.call-start = ((), (), s32[]{:S(2)}) async-start(), calls=%async_computation.6 | async-start | bytes 4194304 | tf_op jit(solution)/shard_map/psum | solution.py:20
  25.4 19.4 %copy-start.11 = (f32[256,512]{1,0:T(8,128)S(1)}, f32[256,512]{1,0:T(8,128)}, u32[]{:S(2)}) copy-start(f32[256,512]{1,0:T(8,128)} %param.38) | copy-start | bytes 1572868
  25.4 19.4 %copy-start.19 = (bf16[256,512]{1,0:T(8,128)(2,1)S(1)}, bf16[256,512]{1,0:T(8,128)(2,1)}, u32[]{:S(2)}) copy-start(bf16[256,512]{1,0:T(8,128)(2,1)} %param.39) | copy-start | bytes 786436
  25.4 20.6 %copy-start.35 = (f32[32,128,32]{1,2,0:T(8,128)S(1)}, f32[32,128,32]{1,2,0:T(8,128)}, u32[]{:S(2)}) copy-start(f32[32,128,32]{1,2,0:T(8,128)} %param.64) | copy-start | bytes 1572868
  43.4 130.1 %all-reduce.22.cloned.1.call-start = ((), (), s32[]{:S(2)}) async-start(), calls=%async_computation.3 | async-start | bytes 6291456 | tf_op jit(solution)/shard_map/psum | solution.py:20
  46.0 74.6 %copy-start.16 = (f32[256,256]{1,0:T(8,128)S(1)}, f32[256,256]{1,0:T(8,128)}, u32[]{:S(2)}) copy-start(f32[256,256]{1,0:T(8,128)} %param.42) | copy-start | bytes 786436
  46.0 74.6 %copy-start.23 = (bf16[256,256]{1,0:T(8,128)(2,1)S(1)}, bf16[256,256]{1,0:T(8,128)(2,1)}, u32[]{:S(2)}) copy-start(bf16[256,256]{1,0:T(8,128)(2,1)} %param.43) | copy-start | bytes 393220
  54.9 66.8 %copy-start.15 = (f32[256,256]{1,0:T(8,128)S(1)}, f32[256,256]{1,0:T(8,128)}, u32[]{:S(2)}) copy-start(f32[256,256]{1,0:T(8,128)} %param.46) | copy-start | bytes 786436
  54.9 66.8 %copy-start.22 = (bf16[256,256]{1,0:T(8,128)(2,1)S(1)}, bf16[256,256]{1,0:T(8,128)(2,1)}, u32[]{:S(2)}) copy-start(bf16[256,256]{1,0:T(8,128)(2,1)} %param.47) | copy-start | bytes 393220
  55.0 65.4 %copy-start.43 = (f32[1,256,32]{1,2,0:T(8,128)S(1)}, f32[1,256,32]{1,2,0:T(8,128)}, u32[]{:S(2)}) copy-start(f32[1,256,32]{1,2,0:T(8,128)} %get-tuple-element.50) | copy-start | bytes 98308
  55.0 66.5 %copy-start.42 = (f32[1,256,32]{1,2,0:T(8,128)S(1)}, f32[1,256,32]{1,2,0:T(8,128)}, u32[]{:S(2)}) copy-start(f32[1,256,32]{1,2,0:T(8,128)} %get-tuple-element.51) | copy-start | bytes 98308
  110.5 260.5 %all-reduce.16.cloned.1.call-start = ((), (), s32[]{:S(2)}) async-start(), calls=%async_computation | async-start | bytes 1048576 | tf_op jit(solution)/shard_map/psum | solution.py:21
  120.6 52.9 %copy-start.27 = (f32[256,32]{0,1:T(8,128)}, f32[256,32]{0,1:T(8,128)S(1)}, u32[]{:S(2)}) copy-start(f32[256,32]{0,1:T(8,128)S(1)} %convolution_bitcast_fusion.13) | copy-start | bytes 98308
  121.7 51.7 %copy-start.29 = (f32[256,32]{0,1:T(8,128)}, f32[256,32]{0,1:T(8,128)S(1)}, u32[]{:S(2)}) copy-start(f32[256,32]{0,1:T(8,128)S(1)} %convolution_bitcast_fusion.10) | copy-start | bytes 98308
  181.1 392.2 %all-reduce.26.cloned.1.call-start = ((), (), s32[]{:S(2)}) async-start(), calls=%async_computation.5 | async-start | bytes 1310720 | tf_op jit(solution)/shard_map/psum | solution.py:20
  515.7 196.3 %copy-start.5 = (f32[32,256,32]{1,2,0:T(8,128)}, f32[32,256,32]{1,2,0:T(8,128)S(1)}, u32[]{:S(2)}) copy-start(f32[32,256,32]{1,2,0:T(8,128)S(1)} %convolution_bitcast_fusion.1) | copy-start | bytes 3145732
  547.3 58.2 %all-reduce.18.cloned.1.call-start = ((), (), s32[]{:S(2)}) async-start(), calls=%async_computation.1 | async-start | bytes 294912 | tf_op jit(solution)/shard_map/psum | solution.py:21
  578.6 117.9 %all-reduce.20.cloned.1.call-start = ((), (), s32[]{:S(2)}) async-start(), calls=%async_computation.2 | async-start | bytes 4718592 | tf_op jit(solution)/shard_map/psum | solution.py:24
  738.8 24.3 %copy-start.31 = (f32[512,64]{0,1:T(8,128)}, f32[512,64]{0,1:T(8,128)S(1)}, u32[]{:S(2)}) copy-start(f32[512,64]{0,1:T(8,128)S(1)} %divide_bitcast_fusion) | copy-start | bytes 393220
  740.6 23.9 %copy-start.40 = (f32[256,32]{0,1:T(8,128)}, f32[256,32]{0,1:T(8,128)S(1)}, u32[]{:S(2)}) copy-start(f32[256,32]{0,1:T(8,128)S(1)} %divide_bitcast_fusion.2) | copy-start | bytes 98308
  741.5 24.2 %copy-start.41 = (f32[256,32]{0,1:T(8,128)}, f32[256,32]{0,1:T(8,128)S(1)}, u32[]{:S(2)}) copy-start(f32[256,32]{0,1:T(8,128)S(1)} %divide_bitcast_fusion.3) | copy-start | bytes 98308
  741.6 25.2 %copy-start.32 = (f32[512,64]{0,1:T(8,128)}, f32[512,64]{0,1:T(8,128)S(1)}, u32[]{:S(2)}) copy-start(f32[512,64]{0,1:T(8,128)S(1)} %divide_bitcast_fusion.1) | copy-start | bytes 393220
  741.6 26.6 %copy-start.1 = (f32[32,256,32]{1,2,0:T(8,128)S(1)}, f32[32,256,32]{1,2,0:T(8,128)}, u32[]{:S(2)}) copy-start(f32[32,256,32]{1,2,0:T(8,128)} %param.56) | copy-start | bytes 3145732
  (29 other events, 387.0 us)
Sparse Core Ops, SparseCore 0:
  11.5 18.1 all-reduce.23
  43.5 59.9 all-reduce.27
  110.6 62.8 all-reduce.21
  181.2 23.1 all-reduce.15
  547.4 25.8 all-reduce.25
  578.8 26.6 all-reduce.17
  646.5 49.9 all-reduce.19
where the time goes:
time: 782 us; the launch traced here: 775 us
  other arithmetic  378 us (48%)
  matrix products  202 us (26%)
  waiting for transfers between devices  144 us (18%)
  blocking collectives  23 us (3%)
  between operations  15.4 us (2%)
  local copies, waits for them, and re-layouts  12.5 us (2%)
    another operation x20, other arithmetic, dion_local(): chol_low = jnp.linalg.cholesky(gram_mat)  302 us
    dot_general x35, matrix products, mat_mul(): jnp.einsum(form, left_op, right_op, preferred_element_type=jnp.float32, p...  190 us
    psum x4, waiting for transfers between devices, dion_local(): p_tilde = lax.psum(mat_mul(forms[0], mom_grad, factor), short_axis)  94.2 us
    another operation x13, other arithmetic, dion_local(): lax.linalg.triangular_solve(chol_low, p_tilde, left_side=False, lower=Tru...  59 us
    psum x1, waiting for transfers between devices, dion_local(): r_new = lax.psum(mat_mul(forms[1], mom_grad, p_orth), long_axis)  35.7 us
  transfers between devices with their start and end apart: 7, of which 5 were waited for; matrix products, arithmetic and copies ran while one was open for 37% of the time, Pallas kernels for 0%

commit v1 on v0

v1 whole, which is shorter than its diff:
```python
import math
import jax
import jax.numpy as jnp
from jax import lax
from jax.experimental import pallas as pl
from jax.experimental.pallas import tpu as pltpu
from jax.sharding import PartitionSpec as P


MOMENTUM = 0.9
LEARN_RATE = 0.3
F32 = jnp.float32
BF = jnp.bfloat16
MESH = pl.DeviceIdType.MESH
NG = 8
PACK = 4
L = 128
H = 256
W = 512
R = 32
RD = 64
COMM_VMEM = 30 << 20
FINAL_VMEM = 30 << 20
SH = 72


def dot(a, b):
    return jnp.dot(a, b, preferred_element_type=F32)


def split3(x):
    a = x.astype(BF)
    r = x - a.astype(F32)
    b = r.astype(BF)
    c = (r - b.astype(F32)).astype(BF)
    return a, b, c


def iota(shape, axis):
    return lax.broadcasted_iota(jnp.int32, shape, axis)


def row_factor(pieces, count, v, rank):
    v1, v2, v3 = split3(v)
    group = iota((1, L), 1) // rank
    acc = acc2 = None
    for m in range(count):
        b12, b1, b3 = pieces(m)
        mask = jnp.where(group == m, 1.0, 0.0).astype(BF)
        w1, w2, w3 = v1 * mask, v2 * mask, v3 * mask
        t = dot(b12, jnp.concatenate([w1, w2], 1))
        u = dot(b1, w3) + dot(b3, w1)
        acc = t if acc is None else acc + t
        acc2 = u if acc2 is None else acc2 + u
    n = acc2.shape[0]
    return acc[:n, :L] + acc2 + (acc[:n, L:] + acc[n:, :L]) + acc[n:, L:]


def col_factor(ut, b1, b2, b3, m, rank):
    lhs = jnp.concatenate([t[rank * m:rank * m + rank] for t in ut], 0)
    o1 = dot(lhs, b1)
    o2 = dot(lhs[:2 * rank], b2)
    o3 = dot(lhs[:rank], b3)
    return o1[:rank] + (o1[rank:2 * rank] + o2[:rank]) + (o1[2 * rank:] + o2[rank:] + o3)


def gram(ut, u, rank):
    full = dot(jnp.concatenate([ut[0], ut[1]], 0), jnp.concatenate([u[0], u[1]], 1))
    low = dot(ut[2], u[0]) + dot(ut[0], u[2])
    g = full[:L, :L] + (full[:L, L:] + full[L:, :L] + low) + full[L:, L:]
    group = iota((rank, L), 1) // rank
    out = jnp.where(group == 0, g[:rank], 0.0)
    for m in range(1, L // rank):
        out = out + jnp.where(group == m, g[rank * m:rank * m + rank], 0.0)
    return out


def inverse_factors(grams, rank):
    lane = iota((rank, L), 1)
    row = iota((rank, L), 0)
    base = (lane // rank) * rank
    col = lane - base
    mats = list(grams)
    for k0 in range(0, rank, 8):
        cols = [[jnp.take_along_axis(a, base + (k0 + j), axis=1) for j in range(8)] for a in mats]
        for j in range(8):
            k = k0 + j
            below = row > k
            for i, a in enumerate(mats):
                ck = cols[i][j]
                factor = jnp.where(below, ck * (1.0 / ck[k:k + 1]), 0.0)
                pivot = jnp.where(col[:1] == k, 1.0, a[k:k + 1])
                mats[i] = jnp.where(below & (col == k), 0.0, a) - factor * pivot
                for l in range(j + 1, 8):
                    cl = cols[i][l]
                    cols[i][l] = cl - factor * cl[k:k + 1]
    out = []
    for a in mats:
        diag = jnp.take_along_axis(a, base + row, axis=1)
        unit = jnp.where(col < row, a, jnp.where(col == row, 1.0, 0.0))
        out.append(unit * (1.0 / jnp.sqrt(diag)))
    return out


def block_diag(inv, rank):
    group = iota((rank, L), 1) // rank
    return jnp.concatenate([jnp.where(group == m, inv, 0.0) for m in range(L // rank)], 0)


def times_right(u, t):
    u1, u2, u3 = split3(u)
    t1, t2, t3 = split3(t)
    t12 = jnp.concatenate([t1, t2], 1)
    a = dot(jnp.concatenate([u1, u2], 1), jnp.concatenate([t12, t12], 0))
    b = dot(jnp.concatenate([u1, u3], 1), jnp.concatenate([t3, t1], 0))
    return a[:, :L] + (a[:, L:] + b)


def times_left(b, v):
    b1, b2, b3 = split3(b)
    v1, v2, v3 = split3(v)
    b12 = jnp.concatenate([b1, b2], 1)
    hi = dot(b12, jnp.concatenate([v1, v1], 0))
    lo = dot(b12, jnp.concatenate([v2, v2], 0))
    lo = lo + dot(jnp.concatenate([b1, b3], 1), jnp.concatenate([v3, v1], 0))
    return hi + lo


def sq_rows_to_lanes(v):
    s = v * v
    f = s[:, :L]
    for i in range(1, v.shape[1] // L):
        f = f + s[:, L * i:L * i + L]
    return jnp.broadcast_to(jnp.sum(f.T, 0, keepdims=True), (8, L))


def sq_lanes(u):
    return jnp.broadcast_to(jnp.sum(u * u, 0, keepdims=True), (8, L))


def gram_to_rows(w, half, rank):
    h = rank // 2
    return jnp.concatenate([w[half * h + 8 * i:half * h + 8 * i + 8] for i in range(h // 8)], 1)


def rows_to_gram(halves, rank):
    parts = []
    for x in halves:
        parts.extend([x[:, L * i:L * i + L] for i in range(rank // 16)])
    return jnp.concatenate(parts, 0)


def comm_kernel(gm, gg, gq, um, ug, uq, dm, dg, dq,
                wqm, wqg, wqf, wkm, wkg, wkf, wvm, wvg, wvf, wom, wog, wof,
                b_e, b_d, b_kv, b_qo, e_inv, e_p, e_rt, e_n, d_r, d_pt, d_n,
                kv_inv, kv_p, kv_rt, kv_n, qo_inv, qo_p, qo_rt, qo_n,
                gs_e, gs_d, qs_e, qs_d, gs_kv, qs_kv, gs_qo, qs_qo,
                z_e, z_d, z_kv, z_qo,
                pown, prcv, down, drc1, dxs, dxr, ptf, sown, src1, sxs, sxr, stf, zown, zrcv,
                nown, nrcv, dnown, dnrcv,
                kpo, kpr, kso, ksr, kxs, kxr, kst, kno, knr,
                qpo, qpr, qso, qsr, qxs, qxr, qst, qno, qnr,
                lsem, dsem, send, recv, sendk, recvk, sendn, recvn):
    tp = lax.axis_index("tp")
    fs = lax.axis_index("fsdp")
    core = lax.rem(fs, 2)
    ypeer = {"tp": 1 - tp}
    sib = {"fsdp": fs + 1 - 2 * core}
    xpeer = {"fsdp": lax.rem(fs + 2, 4)}

    def loads(g):
        s = lax.rem(g, 2)
        e = pl.ds(g * PACK, PACK)
        pairs = [(gm.at[e], b_e.at[0, e]), (gg.at[e], gs_e.at[s, 0]), (gq.at[e], qs_e.at[s, 0]),
                 (um.at[e], b_e.at[1, e]), (ug.at[e], gs_e.at[s, 1]), (uq.at[e], qs_e.at[s, 1])]
        return [pltpu.make_async_copy(a, b, lsem.at[s, i]) for i, (a, b) in enumerate(pairs)]

    def loads_down(g):
        s = lax.rem(g, 2)
        e = pl.ds(g * PACK, PACK)
        pairs = [(dm.at[e], b_d.at[e]), (dg.at[e], gs_d.at[s]), (dq.at[e], qs_d.at[s])]
        return [pltpu.make_async_copy(a, b, lsem.at[s, len(pairs) * 2 + i]) for i, (a, b) in enumerate(pairs)]

    dense_loads = [pltpu.make_async_copy(a, b, dsem.at[i]) for i, (a, b) in enumerate([
        (wkm, b_kv.at[0]), (wkg, gs_kv.at[0]), (wkf, qs_kv.at[0]),
        (wvm, b_kv.at[1]), (wvg, gs_kv.at[1]), (wvf, qs_kv.at[1]),
        (wqm, b_qo.at[0]), (wqg, gs_qo.at[0]), (wqf, qs_qo.at[0]),
        (wom, b_qo.at[1]), (wog, gs_qo.at[1]), (wof, qs_qo.at[1])])]
    for c in dense_loads:
        c.start()

    barrier = pltpu.get_barrier_semaphore()
    fours = [{"fsdp": lax.rem(fs + i, 4)} for i in (1, 2, 3)]
    for dev in [ypeer] + fours:
        pl.semaphore_signal(barrier, inc=1, device_id=dev, device_id_type=MESH)
    pl.semaphore_wait(barrier, 4)

    def remote(src, dst, ss, rs, dev):
        return pltpu.make_async_remote_copy(src_ref=src, dst_ref=dst, send_sem=ss, recv_sem=rs,
                                            device_id=dev, device_id_type=MESH)

    def c_p(g, q):
        return remote(pown.at[lax.rem(g, 2), q], prcv.at[g, q], send.at[q, g], recv.at[q, g], ypeer)

    def c_d1(g):
        return remote(down.at[lax.rem(g, 2), 1 - core], drc1.at[g], send.at[2, g], recv.at[2, g], sib)

    def c_d2(g):
        return remote(dxs.at[lax.rem(g, 2)], dxr.at[g], send.at[3, g], recv.at[3, g], xpeer)

    def c_d3(g):
        return remote(ptf.at[g, core], ptf.at[g, core], send.at[4, g], recv.at[4, g], sib)

    def c_s1(g):
        return remote(sown.at[lax.rem(g, 2), 1 - core], src1.at[g], send.at[5, g], recv.at[5, g], sib)

    def c_s2(g):
        return remote(sxs.at[lax.rem(g, 2)], sxr.at[g], send.at[6, g], recv.at[6, g], xpeer)

    def c_s3(g):
        return remote(stf.at[g, core], stf.at[g, core], send.at[7, g], recv.at[7, g], sib)

    def c_z(g):
        return remote(zown.at[lax.rem(g, 2)], zrcv.at[g], send.at[8, g], recv.at[8, g], ypeer)

    def c_n(g):
        return remote(nown.at[g], nrcv.at[g], send.at[9, g], recv.at[9, g], ypeer)

    def c_nd(g):
        return [remote(dnown.at[g], dnrcv.at[g, i], sendn.at[i, g], recvn.at[i, g], fours[i]) for i in range(3)]

    def dense_copies(i, po, pr, so, sr, xs, xr, st, no, nr):
        k = lambda j: (sendk.at[i, j], recvk.at[i, j])
        return (lambda: remote(po, pr, *k(0), ypeer),
                lambda: remote(so.at[1 - core], sr, *k(1), sib),
                lambda: remote(xs, xr, *k(2), xpeer),
                lambda: remote(st.at[core], st.at[core], *k(3), sib),
                lambda: remote(no, nr, *k(4), ypeer))

    kc = dense_copies(0, kpo, kpr, kso, ksr, kxs, kxr, kst, kno, knr)
    qc = dense_copies(1, qpo, qpr, qso, qsr, qxs, qxr, qst, qno, qnr)

    def terms(b_ref, g_ref, z_ref):
        for r0 in range(0, b_ref.shape[0], RD):
            rs = pl.ds(r0, RD)
            b = b_ref[rs]
            if g_ref is not None:
                b = b + g_ref[rs].astype(F32)
                b_ref[rs] = b
            b1, b2, b3 = split3(b)
            z_ref[0, rs] = b1
            z_ref[1, rs] = b2
            z_ref[2, rs] = b3

    def pieces_of(z_ref):
        n, w = z_ref.shape[1:]
        return z_ref[0:2].reshape(2 * n, w), z_ref[0], z_ref[2]

    def stage1(g):
        s = lax.rem(g, 2)
        for c in loads(g):
            c.wait()

        def one(q, _):
            for m in range(PACK):
                terms(b_e.at[q, g * PACK + m], gs_e.at[s, q, m], z_e.at[m])
            v = qs_e[s, q].reshape(L, H).T
            pown[s, q] = row_factor(lambda m: pieces_of(z_e.at[m]), PACK, v, R)
            c_p(g, q).start()
            return 0

        lax.fori_loop(0, 2, one, 0)

    def stage1_down(g):
        s = lax.rem(g, 2)
        for c in loads_down(g):
            c.wait()
        ut = split3(qs_d[s].reshape(L, L))
        for m in range(PACK):
            terms(b_d.at[g * PACK + m], gs_d.at[s, m], z_d.at[m])
            part = col_factor(ut, z_d[m, 0], z_d[m, 1], z_d[m, 2], m, R)
            down[s, 0, pl.ds(R * m, R)] = part[:, :H]
            down[s, 1, pl.ds(R * m, R)] = part[:, H:]
        c_d1(g).start()

    def stage1_dense():
        for c in dense_loads:
            c.wait()
        for c in loads_down(0) + loads(0) + loads_down(1):
            c.start()
        for i in range(2):
            terms(b_kv.at[i], gs_kv.at[i], z_kv.at[i])
            terms(b_qo.at[i], gs_qo.at[i], z_qo.at[i])
        v = jnp.concatenate([qs_kv[0], qs_kv[1], qs_kv[0], qs_kv[1]], 0).T
        kpo[:] = row_factor(lambda m: pieces_of(z_kv.at[m % 2]), 4, v, R)
        kc[0]().start()
        v = qs_qo[:].reshape(L, W).T
        qpo[:] = row_factor(lambda m: pieces_of(z_qo.at[m]), 2, v, RD)
        qc[0]().start()

    def stage2a(g):
        s = lax.rem(g, 2)
        c_d1(g).wait()
        dxs[s] = down[s, core] + drc1[g]
        c_d2(g).start()

    def stage2b(g):
        c_d2(g).wait()
        ptf[g, core] = dxs[lax.rem(g, 2)] + dxr[g]
        c_d3(g).start()

    def s_and_gram(u, rank, count, z_of, so):
        ut = u.T
        up, utp = split3(u), split3(ut)
        half = L // rank // 2
        for m in range(count):
            z = z_of(m)
            so[m // half, pl.ds(rank * (m % half), rank)] = col_factor(utp, z[0], z[1], z[2], m, rank)
        w = gram(utp, up, rank)
        for h in range(2):
            so[h, pl.ds(RD, 8)] = gram_to_rows(w, h, rank)

    def stage2c(g):
        s = lax.rem(g, 2)

        def one(q, _):
            c_p(g, q).wait()
            u = pown[s, q] + prcv[g, q]
            e_p[g, q] = u
            for m in range(PACK):
                terms(b_e.at[q, g * PACK + m], None, z_e.at[m])
            s_and_gram(u, R, PACK, z_e.at.__getitem__, sown.at[s, :, q])
            return 0

        lax.fori_loop(0, 2, one, 0)
        c_s1(g).start()

    def stage2c_down(g):
        s = lax.rem(g, 2)
        for m in range(PACK):
            terms(b_d.at[g * PACK + m], None, z_d.at[m])
        c_d3(g).wait()
        vt = jnp.concatenate([ptf[g, 0], ptf[g, 1]], 1)
        d_pt[g] = vt
        v = vt.T
        zown[s, pl.ds(0, L)] = row_factor(lambda m: pieces_of(z_d.at[m]), PACK, v, R)
        zown[s, pl.ds(L, R)] = gram(split3(vt), split3(v), R)
        c_z(g).start()

    def stage2_dense():
        kc[0]().wait()
        u = kpo[:] + kpr[:]
        kv_p[:] = u
        s_and_gram(u, R, 4, lambda m: z_kv.at[m % 2], kso)
        kc[1]().start()
        qc[0]().wait()
        u = qpo[:] + qpr[:]
        qo_p[:] = u
        s_and_gram(u, RD, 2, lambda m: z_qo.at[m], qso)
        qc[1]().start()

    def stage3a(g):
        s = lax.rem(g, 2)
        c_s1(g).wait()
        sxs[s] = sown[s, core] + src1[g]
        c_s2(g).start()

    def stage3b(g):
        c_s2(g).wait()
        stf[g, core] = sxs[lax.rem(g, 2)] + sxr[g]
        c_s3(g).start()

    def stage3a_dense():
        for cs, so, sr, xs in ((kc, kso, ksr, kxs), (qc, qso, qsr, qxs)):
            cs[1]().wait()
            xs[:] = so[core] + sr[:]
            cs[2]().start()

    def stage3b_dense():
        for cs, xs, xr, st in ((kc, kxs, kxr, kst), (qc, qxs, qxr, qst)):
            cs[2]().wait()
            st[core] = xs[:] + xr[:]
            cs[3]().start()

    def apply_keep(rt_ref, n_ref, inv, st, rank):
        bd = block_diag(inv, rank)
        vt = jnp.concatenate([st[0, pl.ds(0, RD)], st[1, pl.ds(0, RD)]], 0)
        rt = times_left(bd, vt)
        rt_ref[:] = rt
        n_ref[:] = sq_rows_to_lanes(rt)

    def stage4(g):
        s = lax.rem(g, 2)
        c_s3(g).wait()
        c_z(g).wait()
        z = zown[s] + zrcv[g]
        ws = [rows_to_gram([stf[g, h, q, pl.ds(RD, 8)] for h in range(2)], R) for q in range(2)]
        inv = inverse_factors(ws + [z[L:]], R)
        for i in range(3):
            e_inv[g, i] = inv[i]
        for q in range(2):
            apply_keep(e_rt.at[g, q], nown.at[g, q], inv[q], stf.at[g, :, q], R)
        c_n(g).start()
        bd = block_diag(inv[2], R)
        r = times_right(z[:L], bd.T)
        d_r[g] = r
        dnown[g] = sq_lanes(r)
        for c in c_nd(g):
            c.start()

    def stage4_dense():
        kc[3]().wait()
        inv = inverse_factors([rows_to_gram([kst[h, pl.ds(RD, 8)] for h in range(2)], R)], R)
        kv_inv[:] = inv[0]
        apply_keep(kv_rt, kno, inv[0], kst, R)
        kc[4]().start()
        qc[3]().wait()
        inv = inverse_factors([rows_to_gram([qst[h, pl.ds(RD, 8)] for h in range(2)], RD)], RD)
        qo_inv[:] = inv[0]
        apply_keep(qo_rt, qno, inv[0], qst, RD)
        qc[4]().start()

    def stage5(g):
        c_n(g).wait()
        for q in range(2):
            e_n[g, q] = 1.0 / jnp.sqrt(nown[g, q] + nrcv[g, q])
        for c in c_nd(g):
            c.wait()
        d_n[g] = 1.0 / jnp.sqrt((dnown[g] + dnrcv[g, 1]) + (dnrcv[g, 0] + dnrcv[g, 2]))

    def stage5_dense():
        kc[4]().wait()
        kv_n[:] = 1.0 / jnp.sqrt(kno[:] + knr[:])
        qc[4]().wait()
        qo_n[:] = 1.0 / jnp.sqrt(qno[:] + qnr[:])

    stage1_dense()
    stage1_down(0)

    def step(t, _):
        def within(lag, stage):
            @pl.when((t >= lag) & (t < NG + lag))
            def _():
                stage(t - lag)

        def only(at, stage):
            @pl.when(t == at)
            def _():
                stage()

        @pl.when(t < NG - 1)
        def _():
            for c in loads(t + 1):
                c.start()

        @pl.when(t < NG - 2)
        def _():
            for c in loads_down(t + 2):
                c.start()

        within(0, stage2a)
        within(0, stage1)

        @pl.when(t < NG - 1)
        def _():
            stage1_down(t + 1)

        within(1, stage2b)
        within(3, stage5)
        only(2, stage5_dense)
        only(0, stage2_dense)
        within(1, stage2c)
        within(2, stage3b)
        only(1, stage3b_dense)
        within(1, stage2c_down)
        within(1, stage3a)
        only(0, stage3a_dense)
        within(2, stage4)
        only(1, stage4_dense)
        return 0

    lax.fori_loop(0, NG + 3, step, 0)


def run_comm(args):
    v = pltpu.VMEM
    dma = pltpu.SemaphoreType.DMA
    out = lambda *shape: v(shape, F32)
    out_shape = [out(2, R, H, H), out(R, L, W), out(2, H, H), out(2, H, W),
                 out(NG, 3, R, L), out(NG, 2, H, L), out(NG, 2, L, H), out(NG, 2, 8, L),
                 out(NG, L, L), out(NG, L, W), out(NG, 8, L),
                 out(R, L), out(H, L), out(L, H), out(8, L),
                 out(RD, L), out(H, L), out(L, W), out(8, L)]

    def pack_bufs(w):
        return [v((H, L), F32), v((H, L), F32), v((2, SH, w), F32), v((SH, w), F32), v((SH, w), F32),
                v((SH, w), F32), v((2, SH, w), F32), v((8, L), F32), v((8, L), F32)]

    scratch = [
        v((2, 2, 4, H, H), BF), v((2, 4, L, W), BF), v((2, 2, 4, R, H), F32), v((2, 4, R, L), F32),
        v((2, H, H), BF), v((2, R, H), F32), v((2, H, W), BF), v((2, RD, W), F32),
        v((4, 3, H, H), BF), v((4, 3, L, W), BF), v((2, 3, H, H), BF), v((2, 3, H, W), BF),
        v((2, 2, H, L), F32), v((NG, 2, H, L), F32),
        v((2, 2, L, H), F32), v((NG, L, H), F32), v((2, L, H), F32), v((NG, L, H), F32),
        v((NG, 2, L, H), F32),
        v((2, 2, 2, SH, H), F32), v((NG, 2, SH, H), F32), v((2, 2, SH, H), F32), v((NG, 2, SH, H), F32),
        v((NG, 2, 2, SH, H), F32),
        v((2, 160, L), F32), v((NG, 160, L), F32),
        v((NG, 2, 8, L), F32), v((NG, 2, 8, L), F32), v((NG, 8, L), F32), v((NG, 3, 8, L), F32),
    ] + pack_bufs(H) + pack_bufs(W) + [
        dma((2, 9)), dma((12,)), dma((10, NG)), dma((10, NG)), dma((2, 5)), dma((2, 5)), dma((3, NG)), dma((3, NG))]
    return pl.pallas_call(
        comm_kernel,
        out_shape=out_shape,
        in_specs=[pl.BlockSpec(memory_space=pl.ANY)] * 21,
        out_specs=[pl.BlockSpec(memory_space=pltpu.VMEM)] * len(out_shape),
        scratch_shapes=scratch,
        name="comm_kernel",
        compiler_params=pltpu.CompilerParams(collective_id=0, has_side_effects=True, vmem_limit_bytes=COMM_VMEM),
    )(*args)


def lane_copies(u, rank):
    count = L // rank
    group = iota((1, L), 1) // rank
    rolled = [u] + [pltpu.roll(u, rank * s, 1) for s in range(1, count)]
    outs = []
    for m in range(count):
        x = rolled[(0 - m) % count]
        for gidx in range(1, count):
            x = jnp.where(group == gidx, rolled[(gidx - m) % count], x)
        outs.append(x)
    return outs


def left_tiles(x, rank):
    a = x.astype(BF)
    r1 = x - a.astype(F32)
    b = r1.astype(BF)
    r2 = r1 - b.astype(F32)
    low = iota((1, L), 1) < RD
    if rank == R:
        return jnp.concatenate([a, jnp.where(low, r1, r2).astype(BF)], 1)
    return jnp.concatenate([a, jnp.where(low, x, r1).astype(BF), jnp.where(low, r1, r2).astype(BF)], 1)


def right_tiles(vt, rank):
    a, b, c = split3(vt)
    if rank == R:
        return jnp.concatenate([a, b, c, jnp.zeros_like(a), a, b, a, b], 0)
    return jnp.concatenate([a, b, c, a, b, a], 0)


def lanes_to_rows(n):
    return jnp.broadcast_to(n[:1], (L, L)).T


def scale_rows(vt, n):
    t = lanes_to_rows(n)
    return jnp.concatenate([vt[:, L * i:L * i + L] * t for i in range(vt.shape[1] // L)], 1)


def keep_update(p0, inv, rt, n, rank, slots, x_of, b_of, xo, mo, qo, step):
    copies = lane_copies(times_right(p0, block_diag(inv, rank).T), rank)
    rts = scale_rows(rt, n)
    for m in slots:
        lhs = left_tiles(copies[m], rank)
        rows = slice(rank * m, rank * m + rank)
        mo(m)[:] = b_of(m)[:] - dot(lhs, right_tiles(rt[rows] * (1.0 - MOMENTUM), rank))
        xo(m)[:] = x_of(m)[:] - dot(lhs, right_tiles(rts[rows] * step, rank))
        qo(m)[:] = rts[rows]


def final_kernel(gx, ux, dx, qx, kx, vx, ox,
                 b_e, b_d, b_kv, b_qo, e_inv, e_p, e_rt, e_n, d_r, d_pt, d_n,
                 kv_inv, kv_p, kv_rt, kv_n, qo_inv, qo_p, qo_rt, qo_n,
                 gxo, gmo, gqo, uxo, umo, uqo, dxo, dmo, dqo,
                 qxo, qmo, qqo, kxo, kmo, kqo, vxo, vmo, vqo, oxo, omo, oqo,
                 xs_kv, xs_qo, mt_kv, mt_qo, qt_kv, qt_qo, isem, osem):
    i = pl.program_id(0)
    step = LEARN_RATE * math.sqrt(2.0)
    ins = [pltpu.make_async_copy(a, b, isem.at[k]) for k, (a, b) in enumerate(
        [(kx, xs_kv.at[0]), (vx, xs_kv.at[1]), (qx, xs_qo.at[0]), (ox, xs_qo.at[1])])]
    outs = [pltpu.make_async_copy(b, a, osem.at[k]) for k, (a, b) in enumerate(
        [(kxo, xs_kv.at[0]), (vxo, xs_kv.at[1]), (qxo, xs_qo.at[0]), (oxo, xs_qo.at[1]),
         (kmo, mt_kv.at[0]), (vmo, mt_kv.at[1]), (qmo, mt_qo.at[0]), (omo, mt_qo.at[1]),
         (kqo, qt_kv.at[0]), (vqo, qt_kv.at[1]), (qqo, qt_qo.at[0]), (oqo, qt_qo.at[1])])]

    @pl.when(i == 0)
    def _():
        for c in ins:
            c.start()

    for q, (x, xo, mo, qo) in enumerate(((gx, gxo, gmo, gqo), (ux, uxo, umo, uqo))):
        keep_update(e_p[i, q], e_inv[i, q], e_rt[i, q], e_n[i, q], R, range(PACK),
                    x.at.__getitem__, lambda m: b_e.at[q, i * PACK + m],
                    xo.at.__getitem__, mo.at.__getitem__, qo.at.__getitem__, step)
    r = d_r[i]
    pt = times_left(block_diag(e_inv[i, 2], R), d_pt[i])
    qpack = r * d_n[i][:1]
    rcopies = lane_copies(r * (1.0 - MOMENTUM), R)
    qcopies = lane_copies(qpack * step, R)
    qrows = qpack.T
    for m in range(PACK):
        rhs = right_tiles(pt[R * m:R * m + R], R)
        dmo[m] = b_d[i * PACK + m] - dot(left_tiles(rcopies[m], R), rhs)
        dxo[m] = dx[m] - dot(left_tiles(qcopies[m], R), rhs)
        dqo[m] = qrows[R * m:R * m + R]

    @pl.when(i == 1)
    def _():
        for c in ins:
            c.wait()
        keep_update(kv_p[:], kv_inv[:], kv_rt[:], kv_n[:], R, range(2),
                    xs_kv.at.__getitem__, b_kv.at.__getitem__,
                    xs_kv.at.__getitem__, mt_kv.at.__getitem__, qt_kv.at.__getitem__, step)
        keep_update(qo_p[:], qo_inv[:], qo_rt[:], qo_n[:], RD, range(2),
                    xs_qo.at.__getitem__, b_qo.at.__getitem__,
                    xs_qo.at.__getitem__, mt_qo.at.__getitem__, qt_qo.at.__getitem__, LEARN_RATE)
        for c in outs:
            c.start()

    @pl.when(i == NG - 1)
    def _():
        for c in outs:
            c.wait()


def run_final(xs, packs):
    hbm = pl.BlockSpec(memory_space=pl.ANY)
    v = pltpu.VMEM

    def spec(a):
        return pl.BlockSpec((PACK,) + a.shape[1:], lambda i: (i, 0, 0))

    out = lambda *shape: jax.ShapeDtypeStruct(shape, F32)
    big = [out(R, H, H), out(R, H, H), out(R, R, H)]
    stacks = big + big + [out(R, L, W), out(R, L, W), out(R, R, L)]
    wide = [out(H, W), out(H, W), out(RD, W)]
    narrow = [out(H, H), out(H, H), out(R, H)]
    return pl.pallas_call(
        final_kernel,
        grid=(NG,),
        out_shape=stacks + wide + narrow + narrow + wide,
        in_specs=[spec(a) for a in xs[:3]] + [hbm] * 4 + [pl.BlockSpec(memory_space=v)] * len(packs),
        out_specs=[spec(a) for a in stacks] + [hbm] * 12,
        scratch_shapes=[v((2, H, H), F32), v((2, H, W), F32), v((2, H, H), F32), v((2, H, W), F32),
                        v((2, R, H), F32), v((2, RD, W), F32),
                        pltpu.SemaphoreType.DMA((4,)), pltpu.SemaphoreType.DMA((12,))],
        name="final_kernel",
        compiler_params=pltpu.CompilerParams(vmem_limit_bytes=FINAL_VMEM, dimension_semantics=("arbitrary",)),
    )(*xs, *packs)


def solution(mesh):
    dense_w = P(('layer', 'fsdp'), 'tp')
    dense_f = P(('layer', 'tp'), None)
    stack_w = P('layer', 'fsdp', 'tp')
    stack_f = P('layer', 'tp', None)
    down_f = P('layer', 'fsdp', None)
    in_specs = (dense_w, dense_w, dense_w, dense_f) * 4 + (stack_w, stack_w, stack_w, stack_f) * 2 + (stack_w, stack_w, stack_w, down_f)
    out_specs = (dense_w, dense_w, dense_f) * 4 + (stack_w, stack_w, stack_f) * 2 + (stack_w, stack_w, down_f)

    def local_step(*b):
        x, m, g = b[0::4], b[1::4], b[2::4]
        q = [jnp.swapaxes(f, -1, -2) for f in b[3::4]]
        comm_in = []
        for i in (4, 5, 6, 0, 1, 2, 3):
            comm_in += [m[i], g[i], q[i]]
        packs = [pltpu.with_memory_space_constraint(a, pltpu.VMEM) for a in run_comm(comm_in)]
        outs = run_final([x[i] for i in (4, 5, 6, 0, 1, 2, 3)], packs)
        outs = list(outs[9:]) + list(outs[:9])
        for i in range(2, 21, 3):
            outs[i] = jnp.swapaxes(outs[i], -1, -2)
        return tuple(outs)

    return jax.shard_map(local_step, mesh=mesh, in_specs=in_specs, out_specs=out_specs, check_vma=False)
```

time: 782 us -> 123 us (0.16)
  other arithmetic: 378 us -> 0 us
  matrix products: 202 us -> 0 us
  waiting for transfers between devices: 144 us -> 0 us
  Pallas kernels: 0 us -> 122 us
  blocking collectives: 23 us -> 0 us
  between operations: 15.4 us -> 0.84 us
  local copies, waits for them, and re-layouts: 12.5 us -> 0 us
    another operation x37 -> x0, other arithmetic: 364 us -> none  [the longest x20 302 us: dion_local(): chol_low = jnp.linalg.cholesky(gram_mat)]
    dot_general x35 -> x0, matrix products: 190 us -> none  [mat_mul(): jnp.einsum(form, left_op, right_op, preferred_element_type=jnp.float32, p...]
    psum x7 -> x0, waiting for transfers between devices: 144 us -> none  [the longest x4 94.2 us: dion_local(): p_tilde = lax.psum(mat_mul(forms[0], mom_grad, factor), short_axis)]
    pallas_call x0 -> x2, Pallas kernels: none -> 122 us  [the longest x1 92 us: run_comm(): pl.pallas_call(comm_kernel, out_shape=out_shape, in_specs=[pl.BlockSpec(m...]
    psum x2 -> x0, blocking collectives: 23 us -> none  [the longest x1 13.8 us: dion_local(): gram_mat = lax.psum(mat_mul('bmr,bms->brs', p_tilde, p_tilde), long_axis)]
    another operation x7 -> x0, matrix products: 12 us -> none  [dion_local(): lax.linalg.triangular_solve(chol_low, p_tilde, left_side=False, lower=Tru...]
  transfers between devices with their start and end apart: 7 -> 0, of which waited for: 5 -> 0; matrix products, arithmetic and copies ran while one was open for 37% -> 0% of each run, Pallas kernels for 0% -> 0%
where the time goes in v1:
time: 123 us
  Pallas kernels  122 us (99%)
    pallas_call x1, Pallas kernels, run_comm(): pl.pallas_call(comm_kernel, out_shape=out_shape, in_specs=[pl.BlockSpec(m...  92 us
    pallas_call x1, Pallas kernels, run_final(): pl.pallas_call(final_kernel, grid=(NG,), out_shape=stacks + wide + narrow...  30.3 us

profile of v1, /device:TPU:0, one launch (start us, length us, event | category | flops | bytes accessed | tf_op | source)
XLA Modules:
  0.0 123.1 jit_solution(5208037815009309075)
XLA Ops:
  0.7 92.0 %comm_kernel.1 = (f32[2,32,256,256]{3,2,1,0:T(8,128)S(1)}, f32[32,128,512]{2,1,0:T(8,128)S(1)}, f32[2,256,256]{2,1,0:T(8,128)S(1)}, f32[2,256,512]{2,1,0:T(8,128...) custom-call(f32[32,256,256]{2,1,0:T(8,128)} %gm.1, ...), custom_call_target="tpu_custom_call" | custom-call | tf_op jit(solution)/shard_map/comm_kernel/pallas_call | solution.py:512
  92.7 30.3 %final_kernel.1 = (f32[32,256,256]{2,1,0:T(8,128)}, f32[32,256,256]{2,1,0:T(8,128)}, f32[32,32,256]{2,1,0:T(8,128)}, f32[32,256,256]{2,1,0:T(8,128)}, f32[32,256...) custom-call(f32[32,256,256]{2,1,0:T(8,128)} %gx.1, ...), custom_call_target="tpu_custom_call" | custom-call | tf_op jit(solution)/shard_map/final_kernel/pallas_call | solution.py:641

commit v2 on v1

--- a/solution.py
+++ b/solution.py
@@ -21,6 +21,7 @@
 RD = 64
 COMM_VMEM = 30 << 20
 FINAL_VMEM = 30 << 20
+NORM_LAG = 4
 SH = 72
 
 
@@ -160,7 +161,7 @@
                 nown, nrcv, dnown, dnrcv,
                 kpo, kpr, kso, ksr, kxs, kxr, kst, kno, knr,
                 qpo, qpr, qso, qsr, qxs, qxr, qst, qno, qnr,
-                lsem, dsem, send, recv, sendk, recvk, sendn, recvn):
+                lsem, dsem, send, recv, sends, recvs, sendk, recvk, sendn, recvn):
     tp = lax.axis_index("tp")
     fs = lax.axis_index("fsdp")
     core = lax.rem(fs, 2)
@@ -211,20 +212,20 @@
     def c_d3(g):
         return remote(ptf.at[g, core], ptf.at[g, core], send.at[4, g], recv.at[4, g], sib)
 
-    def c_s1(g):
-        return remote(sown.at[lax.rem(g, 2), 1 - core], src1.at[g], send.at[5, g], recv.at[5, g], sib)
-
-    def c_s2(g):
-        return remote(sxs.at[lax.rem(g, 2)], sxr.at[g], send.at[6, g], recv.at[6, g], xpeer)
-
-    def c_s3(g):
-        return remote(stf.at[g, core], stf.at[g, core], send.at[7, g], recv.at[7, g], sib)
+    def c_s1(g, q):
+        return remote(sown.at[lax.rem(g, 2), 1 - core, q], src1.at[g, q], sends.at[0, q, g], recvs.at[0, q, g], sib)
+
+    def c_s2(g, q):
+        return remote(sxs.at[lax.rem(g, 2), q], sxr.at[g, q], sends.at[1, q, g], recvs.at[1, q, g], xpeer)
+
+    def c_s3(g, q):
+        return remote(stf.at[g, core, q], stf.at[g, core, q], sends.at[2, q, g], recvs.at[2, q, g], sib)
 
     def c_z(g):
-        return remote(zown.at[lax.rem(g, 2)], zrcv.at[g], send.at[8, g], recv.at[8, g], ypeer)
+        return remote(zown.at[lax.rem(g, 2)], zrcv.at[g], send.at[5, g], recv.at[5, g], ypeer)
 
     def c_n(g):
-        return remote(nown.at[g], nrcv.at[g], send.at[9, g], recv.at[9, g], ypeer)
+        return remote(nown.at[g], nrcv.at[g], send.at[6, g], recv.at[6, g], ypeer)
 
     def c_nd(g):
         return [remote(dnown.at[g], dnrcv.at[g, i], sendn.at[i, g], recvn.at[i, g], fours[i]) for i in range(3)]
@@ -283,17 +284,23 @@
             down[s, 1, pl.ds(R * m, R)] = part[:, H:]
         c_d1(g).start()
 
+    low = iota((1, L), 1) < RD
+
     def stage1_dense():
-        for c in dense_loads:
+        for c in dense_loads[:6]:
+            c.wait()
+        for i in range(2):
+            terms(b_kv.at[i], gs_kv.at[i], z_kv.at[i])
+        v = jnp.concatenate([qs_kv[0], qs_kv[1], qs_kv[0], qs_kv[1]], 0).T
+        u = row_factor(lambda m: pieces_of(z_kv.at[m % 2]), 4, v, R)
+        kpo[:] = jnp.where(low, u[:L], u[L:])
+        kc[0]().start()
+        for c in dense_loads[6:]:
             c.wait()
         for c in loads_down(0) + loads(0) + loads_down(1):
             c.start()
         for i in range(2):
-            terms(b_kv.at[i], gs_kv.at[i], z_kv.at[i])
             terms(b_qo.at[i], gs_qo.at[i], z_qo.at[i])
-        v = jnp.concatenate([qs_kv[0], qs_kv[1], qs_kv[0], qs_kv[1]], 0).T
-        kpo[:] = row_factor(lambda m: pieces_of(z_kv.at[m % 2]), 4, v, R)
-        kc[0]().start()
         v = qs_qo[:].reshape(L, W).T
         qpo[:] = row_factor(lambda m: pieces_of(z_qo.at[m]), 2, v, RD)
         qc[0]().start()
@@ -330,10 +337,10 @@
             for m in range(PACK):
                 terms(b_e.at[q, g * PACK + m], None, z_e.at[m])
             s_and_gram(u, R, PACK, z_e.at.__getitem__, sown.at[s, :, q])
+            c_s1(g, q).start()
             return 0
 
         lax.fori_loop(0, 2, one, 0)
-        c_s1(g).start()
 
     def stage2c_down(g):
         s = lax.rem(g, 2)
@@ -350,6 +357,8 @@
     def stage2_dense():
         kc[0]().wait()
         u = kpo[:] + kpr[:]
+        t = pltpu.roll(u, RD, 1)
+        u = jnp.concatenate([jnp.where(low, u, t), jnp.where(low, t, u)], 0)
         kv_p[:] = u
         s_and_gram(u, R, 4, lambda m: z_kv.at[m % 2], kso)
         kc[1]().start()
@@ -359,16 +368,17 @@
         s_and_gram(u, RD, 2, lambda m: z_qo.at[m], qso)
         qc[1]().start()
 
-    def stage3a(g):
-        s = lax.rem(g, 2)
-        c_s1(g).wait()
-        sxs[s] = sown[s, core] + src1[g]
-        c_s2(g).start()
+    def stage3a(g, q):
+        s = lax.rem(g, 2)
+        c_s1(g, q).wait()
+        sxs[s, q] = sown[s, core, q] + src1[g, q]
+        c_s2(g, q).start()
 
     def stage3b(g):
-        c_s2(g).wait()
-        stf[g, core] = sxs[lax.rem(g, 2)] + sxr[g]
-        c_s3(g).start()
+        for q in range(2):
+            c_s2(g, q).wait()
+            stf[g, core, q] = sxs[lax.rem(g, 2), q] + sxr[g, q]
+            c_s3(g, q).start()
 
     def stage3a_dense():
         for cs, so, sr, xs in ((kc, kso, ksr, kxs), (qc, qso, qsr, qxs)):
@@ -391,7 +401,8 @@
 
     def stage4(g):
         s = lax.rem(g, 2)
-        c_s3(g).wait()
+        for q in range(2):
+            c_s3(g, q).wait()
         c_z(g).wait()
         z = zown[s] + zrcv[g]
         ws = [rows_to_gram([stf[g, h, q, pl.ds(RD, 8)] for h in range(2)], R) for q in range(2)]
@@ -466,20 +477,23 @@
             stage1_down(t + 1)
 
         within(1, stage2b)
-        within(3, stage5)
-        only(2, stage5_dense)
+        within(NORM_LAG, stage5)
+        only(3, stage5_dense)
         only(0, stage2_dense)
         within(1, stage2c)
+        within(1, lambda g: stage3a(g, 0))
         within(2, stage3b)
         only(1, stage3b_dense)
         within(1, stage2c_down)
-        within(1, stage3a)
+        within(1, lambda g: stage3a(g, 1))
         only(0, stage3a_dense)
         within(2, stage4)
         only(1, stage4_dense)
         return 0
 
-    lax.fori_loop(0, NG + 3, step, 0)
+    lax.fori_loop(0, NG + 2, step, 0)
+    for g in range(NG + 2 - NORM_LAG, NG):
+        stage5(g)
 
 
 def run_comm(args):
@@ -492,8 +506,8 @@
                  out(R, L), out(H, L), out(L, H), out(8, L),
                  out(RD, L), out(H, L), out(L, W), out(8, L)]
 
-    def pack_bufs(w):
-        return [v((H, L), F32), v((H, L), F32), v((2, SH, w), F32), v((SH, w), F32), v((SH, w), F32),
+    def pack_bufs(rows, w):
+        return [v((rows, L), F32), v((rows, L), F32), v((2, SH, w), F32), v((SH, w), F32), v((SH, w), F32),
                 v((SH, w), F32), v((2, SH, w), F32), v((8, L), F32), v((8, L), F32)]
 
     scratch = [
@@ -507,8 +521,8 @@
         v((NG, 2, 2, SH, H), F32),
         v((2, 160, L), F32), v((NG, 160, L), F32),
         v((NG, 2, 8, L), F32), v((NG, 2, 8, L), F32), v((NG, 8, L), F32), v((NG, 3, 8, L), F32),
-    ] + pack_bufs(H) + pack_bufs(W) + [
-        dma((2, 9)), dma((12,)), dma((10, NG)), dma((10, NG)), dma((2, 5)), dma((2, 5)), dma((3, NG)), dma((3, NG))]
+    ] + pack_bufs(L, H) + pack_bufs(H, W) + [
+        dma((2, 9)), dma((12,)), dma((7, NG)), dma((7, NG)), dma((3, 2, NG)), dma((3, 2, NG)), dma((2, 5)), dma((2, 5)), dma((3, NG)), dma((3, NG))]
     return pl.pallas_call(
         comm_kernel,
         out_shape=out_shape,
@@ -566,8 +580,11 @@
     for m in slots:
         lhs = left_tiles(copies[m], rank)
         rows = slice(rank * m, rank * m + rank)
-        mo(m)[:] = b_of(m)[:] - dot(lhs, right_tiles(rt[rows] * (1.0 - MOMENTUM), rank))
-        xo(m)[:] = x_of(m)[:] - dot(lhs, right_tiles(rts[rows] * step, rank))
+        both = right_tiles(jnp.concatenate([rt[rows] * (1.0 - MOMENTUM), rts[rows] * step], 1), rank)
+        out = dot(lhs, both)
+        n_cols = rt.shape[1]
+        mo(m)[:] = b_of(m)[:] - out[:, :n_cols]
+        xo(m)[:] = x_of(m)[:] - out[:, n_cols:]
         qo(m)[:] = rts[rows]
 
 
@@ -603,8 +620,9 @@
     qrows = qpack.T
     for m in range(PACK):
         rhs = right_tiles(pt[R * m:R * m + R], R)
-        dmo[m] = b_d[i * PACK + m] - dot(left_tiles(rcopies[m], R), rhs)
-        dxo[m] = dx[m] - dot(left_tiles(qcopies[m], R), rhs)
+        out = dot(jnp.concatenate([left_tiles(rcopies[m], R), left_tiles(qcopies[m], R)], 0), rhs)
+        dmo[m] = b_d[i * PACK + m] - out[:L]
+        dxo[m] = dx[m] - out[L:]
         dqo[m] = qrows[R * m:R * m + R]
 
     @pl.when(i == 1)

time: 123 us -> 114 us (0.927)
  Pallas kernels: 122 us -> 113 us
    pallas_call x1, Pallas kernels: 92 us -> 82.6 us  [run_comm(): pl.pallas_call(comm_kernel, out_shape=out_shape, in_specs=[pl.BlockSpec(m...]
where the time goes in v2:
time: 114 us
  Pallas kernels  113 us (99%)
    pallas_call x1, Pallas kernels, run_comm(): pl.pallas_call(comm_kernel, out_shape=out_shape, in_specs=[pl.BlockSpec(m...  82.6 us
    pallas_call x1, Pallas kernels, run_final(): pl.pallas_call(final_kernel, grid=(NG,), out_shape=stacks + wide + narrow...  30.1 us

profile of v2, /device:TPU:0, one launch (start us, length us, event | category | flops | bytes accessed | tf_op | source)
XLA Modules:
  0.0 113.6 jit_solution(917671588119804754)
XLA Ops:
  0.7 82.6 %comm_kernel.1 = (f32[2,32,256,256]{3,2,1,0:T(8,128)S(1)}, f32[32,128,512]{2,1,0:T(8,128)S(1)}, f32[2,256,256]{2,1,0:T(8,128)S(1)}, f32[2,256,512]{2,1,0:T(8,128...) custom-call(f32[32,256,256]{2,1,0:T(8,128)} %gm.1, ...), custom_call_target="tpu_custom_call" | custom-call | tf_op jit(solution)/shard_map/comm_kernel/pallas_call | solution.py:526
  83.3 30.1 %final_kernel.1 = (f32[32,256,256]{2,1,0:T(8,128)}, f32[32,256,256]{2,1,0:T(8,128)}, f32[32,32,256]{2,1,0:T(8,128)}, f32[32,256,256]{2,1,0:T(8,128)}, f32[32,256...) custom-call(f32[32,256,256]{2,1,0:T(8,128)} %gx.1, ...), custom_call_target="tpu_custom_call" | custom-call | tf_op jit(solution)/shard_map/final_kernel/pallas_call | solution.py:659

commit v3 on v2

--- a/solution.py
+++ b/solution.py
@@ -19,9 +19,12 @@
 W = 512
 R = 32
 RD = 64
-COMM_VMEM = 30 << 20
-FINAL_VMEM = 30 << 20
+COMM_VMEM = 22 << 20
+FINAL_VMEM = 22 << 20
 NORM_LAG = 4
+OUT_SLOTS = 3
+IN_SLOTS = 4
+TWO = 2
 SH = 72
 
 
@@ -152,12 +155,12 @@
 
 
 def comm_kernel(gm, gg, gq, um, ug, uq, dm, dg, dq,
-                wqm, wqg, wqf, wkm, wkg, wkf, wvm, wvg, wvf, wom, wog, wof,
-                b_e, b_d, b_kv, b_qo, e_inv, e_p, e_rt, e_n, d_r, d_pt, d_n,
+                wqm, wqg, wqf, wkm, wkg, wkf, wvm, wvg, wvf, wom, wog, wof, gx,
+                x_g, b_e, b_d, b_kv, b_qo, e_inv, e_p, e_rt, e_n, d_r, d_pt, d_n,
                 kv_inv, kv_p, kv_rt, kv_n, qo_inv, qo_p, qo_rt, qo_n,
                 gs_e, gs_d, qs_e, qs_d, gs_kv, qs_kv, gs_qo, qs_qo,
                 z_e, z_d, z_kv, z_qo,
-                pown, prcv, down, drc1, dxs, dxr, ptf, sown, src1, sxs, sxr, stf, zown, zrcv,
+                pown, prcv, down, drc1, dxs, dxr, sown, src1, sxs, sxr, stf, zown, zrcv,
                 nown, nrcv, dnown, dnrcv,
                 kpo, kpr, kso, ksr, kxs, kxr, kst, kno, knr,
                 qpo, qpr, qso, qsr, qxs, qxr, qst, qno, qnr,
@@ -187,6 +190,7 @@
         (wvm, b_kv.at[1]), (wvg, gs_kv.at[1]), (wvf, qs_kv.at[1]),
         (wqm, b_qo.at[0]), (wqg, gs_qo.at[0]), (wqf, qs_qo.at[0]),
         (wom, b_qo.at[1]), (wog, gs_qo.at[1]), (wof, qs_qo.at[1])])]
+    x_load = pltpu.make_async_copy(gx, x_g, dsem.at[len(dense_loads)])
     for c in dense_loads:
         c.start()
 
@@ -201,28 +205,28 @@
                                             device_id=dev, device_id_type=MESH)
 
     def c_p(g, q):
-        return remote(pown.at[lax.rem(g, 2), q], prcv.at[g, q], send.at[q, g], recv.at[q, g], ypeer)
+        return remote(pown.at[lax.rem(g, 2), q], prcv.at[lax.rem(g, 3), q], send.at[q, g], recv.at[q, g], ypeer)
 
     def c_d1(g):
-        return remote(down.at[lax.rem(g, 2), 1 - core], drc1.at[g], send.at[2, g], recv.at[2, g], sib)
+        return remote(down.at[lax.rem(g, 2), 1 - core], drc1.at[lax.rem(g, 2)], send.at[2, g], recv.at[2, g], sib)
 
     def c_d2(g):
-        return remote(dxs.at[lax.rem(g, 2)], dxr.at[g], send.at[3, g], recv.at[3, g], xpeer)
+        return remote(dxs.at[lax.rem(g, 2)], dxr.at[lax.rem(g, 3)], send.at[3, g], recv.at[3, g], xpeer)
 
     def c_d3(g):
-        return remote(ptf.at[g, core], ptf.at[g, core], send.at[4, g], recv.at[4, g], sib)
+        return remote(d_pt.at[g, core], d_pt.at[g, core], send.at[4, g], recv.at[4, g], sib)
 
     def c_s1(g, q):
-        return remote(sown.at[lax.rem(g, 2), 1 - core, q], src1.at[g, q], sends.at[0, q, g], recvs.at[0, q, g], sib)
+        return remote(sown.at[lax.rem(g, 2), 1 - core, q], src1.at[lax.rem(g, 2), q], sends.at[0, q, g], recvs.at[0, q, g], sib)
 
     def c_s2(g, q):
-        return remote(sxs.at[lax.rem(g, 2), q], sxr.at[g, q], sends.at[1, q, g], recvs.at[1, q, g], xpeer)
+        return remote(sxs.at[lax.rem(g, 2), q], sxr.at[lax.rem(g, 3), q], sends.at[1, q, g], recvs.at[1, q, g], xpeer)
 
     def c_s3(g, q):
-        return remote(stf.at[g, core, q], stf.at[g, core, q], sends.at[2, q, g], recvs.at[2, q, g], sib)
+        return remote(stf.at[lax.rem(g, 2), core, q], stf.at[lax.rem(g, 2), core, q], sends.at[2, q, g], recvs.at[2, q, g], sib)
 
     def c_z(g):
-        return remote(zown.at[lax.rem(g, 2)], zrcv.at[g], send.at[5, g], recv.at[5, g], ypeer)
+        return remote(zown.at[lax.rem(g, 2)], zrcv.at[lax.rem(g, 3)], send.at[5, g], recv.at[5, g], ypeer)
 
     def c_n(g):
         return remote(nown.at[g], nrcv.at[g], send.at[6, g], recv.at[6, g], ypeer)
@@ -308,12 +312,12 @@
     def stage2a(g):
         s = lax.rem(g, 2)
         c_d1(g).wait()
-        dxs[s] = down[s, core] + drc1[g]
+        dxs[s] = down[s, core] + drc1[s]
         c_d2(g).start()
 
     def stage2b(g):
         c_d2(g).wait()
-        ptf[g, core] = dxs[lax.rem(g, 2)] + dxr[g]
+        d_pt[g, core] = dxs[lax.rem(g, 2)] + dxr[lax.rem(g, 3)]
         c_d3(g).start()
 
     def s_and_gram(u, rank, count, z_of, so):
@@ -332,7 +336,7 @@
 
         def one(q, _):
             c_p(g, q).wait()
-            u = pown[s, q] + prcv[g, q]
+            u = pown[s, q] + prcv[lax.rem(g, 3), q]
             e_p[g, q] = u
             for m in range(PACK):
                 terms(b_e.at[q, g * PACK + m], None, z_e.at[m])
@@ -347,8 +351,7 @@
         for m in range(PACK):
             terms(b_d.at[g * PACK + m], None, z_d.at[m])
         c_d3(g).wait()
-        vt = jnp.concatenate([ptf[g, 0], ptf[g, 1]], 1)
-        d_pt[g] = vt
+        vt = jnp.concatenate([d_pt[g, 0], d_pt[g, 1]], 1)
         v = vt.T
         zown[s, pl.ds(0, L)] = row_factor(lambda m: pieces_of(z_d.at[m]), PACK, v, R)
         zown[s, pl.ds(L, R)] = gram(split3(vt), split3(v), R)
@@ -371,13 +374,13 @@
     def stage3a(g, q):
         s = lax.rem(g, 2)
         c_s1(g, q).wait()
-        sxs[s, q] = sown[s, core, q] + src1[g, q]
+        sxs[s, q] = sown[s, core, q] + src1[s, q]
         c_s2(g, q).start()
 
     def stage3b(g):
         for q in range(2):
             c_s2(g, q).wait()
-            stf[g, core, q] = sxs[lax.rem(g, 2), q] + sxr[g, q]
+            stf[lax.rem(g, 2), core, q] = sxs[lax.rem(g, 2), q] + sxr[lax.rem(g, 3), q]
             c_s3(g, q).start()
 
     def stage3a_dense():
@@ -404,13 +407,13 @@
         for q in range(2):
             c_s3(g, q).wait()
         c_z(g).wait()
-        z = zown[s] + zrcv[g]
-        ws = [rows_to_gram([stf[g, h, q, pl.ds(RD, 8)] for h in range(2)], R) for q in range(2)]
+        z = zown[s] + zrcv[lax.rem(g, 3)]
+        ws = [rows_to_gram([stf[s, h, q, pl.ds(RD, 8)] for h in range(2)], R) for q in range(2)]
         inv = inverse_factors(ws + [z[L:]], R)
         for i in range(3):
             e_inv[g, i] = inv[i]
         for q in range(2):
-            apply_keep(e_rt.at[g, q], nown.at[g, q], inv[q], stf.at[g, :, q], R)
+            apply_keep(e_rt.at[g, q], nown.at[g, q], inv[q], stf.at[s, :, q], R)
         c_n(g).start()
         bd = block_diag(inv[2], R)
         r = times_right(z[:L], bd.T)
@@ -469,6 +472,7 @@
             for c in loads_down(t + 2):
                 c.start()
 
+        only(2, x_load.start)
         within(0, stage2a)
         within(0, stage1)
 
@@ -492,6 +496,7 @@
         return 0
 
     lax.fori_loop(0, NG + 2, step, 0)
+    x_load.wait()
     for g in range(NG + 2 - NORM_LAG, NG):
         stage5(g)
 
@@ -500,33 +505,32 @@
     v = pltpu.VMEM
     dma = pltpu.SemaphoreType.DMA
     out = lambda *shape: v(shape, F32)
-    out_shape = [out(2, R, H, H), out(R, L, W), out(2, H, H), out(2, H, W),
-                 out(NG, 3, R, L), out(NG, 2, H, L), out(NG, 2, L, H), out(NG, 2, 8, L),
-                 out(NG, L, L), out(NG, L, W), out(NG, 8, L),
+    out_shape = [out(R, H, H), out(2, R, H, H), out(R, L, W), out(2, H, H), out(2, H, W),
+                 out(NG, 3, R, L), out(NG, TWO, H, L), out(NG, TWO, L, H), out(NG, TWO, 8, L),
+                 out(NG, L, L), out(NG, TWO, L, H), out(NG, 8, L),
                  out(R, L), out(H, L), out(L, H), out(8, L),
                  out(RD, L), out(H, L), out(L, W), out(8, L)]
 
     def pack_bufs(rows, w):
-        return [v((rows, L), F32), v((rows, L), F32), v((2, SH, w), F32), v((SH, w), F32), v((SH, w), F32),
-                v((SH, w), F32), v((2, SH, w), F32), v((8, L), F32), v((8, L), F32)]
+        return [v((rows, L), F32), v((rows, L), F32), v((TWO, SH, w), F32), v((SH, w), F32), v((SH, w), F32),
+                v((SH, w), F32), v((TWO, SH, w), F32), v((8, L), F32), v((8, L), F32)]
 
     scratch = [
-        v((2, 2, 4, H, H), BF), v((2, 4, L, W), BF), v((2, 2, 4, R, H), F32), v((2, 4, R, L), F32),
-        v((2, H, H), BF), v((2, R, H), F32), v((2, H, W), BF), v((2, RD, W), F32),
-        v((4, 3, H, H), BF), v((4, 3, L, W), BF), v((2, 3, H, H), BF), v((2, 3, H, W), BF),
-        v((2, 2, H, L), F32), v((NG, 2, H, L), F32),
-        v((2, 2, L, H), F32), v((NG, L, H), F32), v((2, L, H), F32), v((NG, L, H), F32),
-        v((NG, 2, L, H), F32),
-        v((2, 2, 2, SH, H), F32), v((NG, 2, SH, H), F32), v((2, 2, SH, H), F32), v((NG, 2, SH, H), F32),
-        v((NG, 2, 2, SH, H), F32),
-        v((2, 160, L), F32), v((NG, 160, L), F32),
+        v((TWO, TWO, 4, H, H), BF), v((TWO, 4, L, W), BF), v((TWO, TWO, 4, R, H), F32), v((TWO, 4, R, L), F32),
+        v((TWO, H, H), BF), v((TWO, R, H), F32), v((TWO, H, W), BF), v((TWO, RD, W), F32),
+        v((4, 3, H, H), BF), v((4, 3, L, W), BF), v((TWO, 3, H, H), BF), v((TWO, 3, H, W), BF),
+        v((TWO, TWO, H, L), F32), v((3, 2, H, L), F32),
+        v((TWO, TWO, L, H), F32), v((TWO, L, H), F32), v((TWO, L, H), F32), v((3, L, H), F32),
+        v((TWO, TWO, TWO, SH, H), F32), v((TWO, TWO, SH, H), F32), v((TWO, TWO, SH, H), F32), v((3, 2, SH, H), F32),
+        v((TWO, TWO, TWO, SH, H), F32),
+        v((TWO, L + R, L), F32), v((3, L + R, L), F32),
         v((NG, 2, 8, L), F32), v((NG, 2, 8, L), F32), v((NG, 8, L), F32), v((NG, 3, 8, L), F32),
     ] + pack_bufs(L, H) + pack_bufs(H, W) + [
-        dma((2, 9)), dma((12,)), dma((7, NG)), dma((7, NG)), dma((3, 2, NG)), dma((3, 2, NG)), dma((2, 5)), dma((2, 5)), dma((3, NG)), dma((3, NG))]
+        dma((2, 9)), dma((13,)), dma((7, NG)), dma((7, NG)), dma((3, 2, NG)), dma((3, 2, NG)), dma((2, 5)), dma((2, 5)), dma((3, NG)), dma((3, NG))]
     return pl.pallas_call(
         comm_kernel,
         out_shape=out_shape,
-        in_specs=[pl.BlockSpec(memory_space=pl.ANY)] * 21,
+        in_specs=[pl.BlockSpec(memory_space=pl.ANY)] * len(args),
         out_specs=[pl.BlockSpec(memory_space=pltpu.VMEM)] * len(out_shape),
         scratch_shapes=scratch,
         name="comm_kernel",
@@ -534,12 +538,12 @@
     )(*args)
 
 
-def lane_copies(u, rank):
+def lane_copies(u, rank, slots):
     count = L // rank
     group = iota((1, L), 1) // rank
     rolled = [u] + [pltpu.roll(u, rank * s, 1) for s in range(1, count)]
     outs = []
-    for m in range(count):
+    for m in slots:
         x = rolled[(0 - m) % count]
         for gidx in range(1, count):
             x = jnp.where(group == gidx, rolled[(gidx - m) % count], x)
@@ -574,27 +578,27 @@
     return jnp.concatenate([vt[:, L * i:L * i + L] * t for i in range(vt.shape[1] // L)], 1)
 
 
-def keep_update(p0, inv, rt, n, rank, slots, x_of, b_of, xo, mo, qo, step):
-    copies = lane_copies(times_right(p0, block_diag(inv, rank).T), rank)
-    rts = scale_rows(rt, n)
-    for m in slots:
-        lhs = left_tiles(copies[m], rank)
+def keep_update(p, rt, rts, rank, x_of, b_of, xo, mo, qo, step):
+    copies = lane_copies(p, rank, range(TWO))
+    n_cols = rt.shape[1]
+    for m in range(TWO):
         rows = slice(rank * m, rank * m + rank)
         both = right_tiles(jnp.concatenate([rt[rows] * (1.0 - MOMENTUM), rts[rows] * step], 1), rank)
-        out = dot(lhs, both)
-        n_cols = rt.shape[1]
+        out = dot(left_tiles(copies[m], rank), both)
         mo(m)[:] = b_of(m)[:] - out[:, :n_cols]
         xo(m)[:] = x_of(m)[:] - out[:, n_cols:]
         qo(m)[:] = rts[rows]
 
 
-def final_kernel(gx, ux, dx, qx, kx, vx, ox,
-                 b_e, b_d, b_kv, b_qo, e_inv, e_p, e_rt, e_n, d_r, d_pt, d_n,
+def final_kernel(ux, dx, qx, kx, vx, ox,
+                 x_g, b_e, b_d, b_kv, b_qo, e_inv, e_p, e_rt, e_n, d_r, d_pt, d_n,
                  kv_inv, kv_p, kv_rt, kv_n, qo_inv, qo_p, qo_rt, qo_n,
                  gxo, gmo, gqo, uxo, umo, uqo, dxo, dmo, dqo,
                  qxo, qmo, qqo, kxo, kmo, kqo, vxo, vmo, vqo, oxo, omo, oqo,
-                 xs_kv, xs_qo, mt_kv, mt_qo, qt_kv, qt_qo, isem, osem):
+                 x_u, x_d, load_sem, out_e, outq_e, out_d, outq_d, stack_sem,
+                 p_s, rts_s, r_s, pt_s, qrow_s, xs_kv, xs_qo, mt_kv, mt_qo, qt_kv, qt_qo, isem, osem):
     i = pl.program_id(0)
+    g, h = i // 2, lax.rem(i, 2)
     step = LEARN_RATE * math.sqrt(2.0)
     ins = [pltpu.make_async_copy(a, b, isem.at[k]) for k, (a, b) in enumerate(
         [(kx, xs_kv.at[0]), (vx, xs_kv.at[1]), (qx, xs_qo.at[0]), (ox, xs_qo.at[1])])]
@@ -603,53 +607,101 @@
          (kmo, mt_kv.at[0]), (vmo, mt_kv.at[1]), (qmo, mt_qo.at[0]), (omo, mt_qo.at[1]),
          (kqo, qt_kv.at[0]), (vqo, qt_kv.at[1]), (qqo, qt_qo.at[0]), (oqo, qt_qo.at[1])])]
 
+    def stack_outs(j):
+        s = lax.rem(j, OUT_SLOTS)
+        e = pl.ds(2 * j, 2)
+        pairs = [(out_e.at[s, 0, 0], gxo), (out_e.at[s, 0, 1], gmo), (outq_e.at[s, 0], gqo),
+                 (out_e.at[s, 1, 0], uxo), (out_e.at[s, 1, 1], umo), (outq_e.at[s, 1], uqo),
+                 (out_d.at[s, 0], dxo), (out_d.at[s, 1], dmo), (outq_d.at[s], dqo)]
+        return [pltpu.make_async_copy(a, b.at[e], stack_sem.at[k, s]) for k, (a, b) in enumerate(pairs)]
+
+    def stack_ins(j):
+        s = lax.rem(j, IN_SLOTS)
+        e = pl.ds(2 * j, 2)
+        return [pltpu.make_async_copy(a.at[e], b.at[s], load_sem.at[k, s]) for k, (a, b) in enumerate(((ux, x_u), (dx, x_d)))]
+
+    slot, ins_slot = lax.rem(i, OUT_SLOTS), lax.rem(i, IN_SLOTS)
+
     @pl.when(i == 0)
     def _():
+        for j in range(IN_SLOTS):
+            for c in stack_ins(j):
+                c.start()
         for c in ins:
             c.start()
 
-    for q, (x, xo, mo, qo) in enumerate(((gx, gxo, gmo, gqo), (ux, uxo, umo, uqo))):
-        keep_update(e_p[i, q], e_inv[i, q], e_rt[i, q], e_n[i, q], R, range(PACK),
-                    x.at.__getitem__, lambda m: b_e.at[q, i * PACK + m],
-                    xo.at.__getitem__, mo.at.__getitem__, qo.at.__getitem__, step)
-    r = d_r[i]
-    pt = times_left(block_diag(e_inv[i, 2], R), d_pt[i])
-    qpack = r * d_n[i][:1]
-    rcopies = lane_copies(r * (1.0 - MOMENTUM), R)
-    qcopies = lane_copies(qpack * step, R)
-    qrows = qpack.T
-    for m in range(PACK):
-        rhs = right_tiles(pt[R * m:R * m + R], R)
-        out = dot(jnp.concatenate([left_tiles(rcopies[m], R), left_tiles(qcopies[m], R)], 0), rhs)
-        dmo[m] = b_d[i * PACK + m] - out[:L]
-        dxo[m] = dx[m] - out[L:]
-        dqo[m] = qrows[R * m:R * m + R]
+    for c in stack_ins(i):
+        c.wait()
+
+    @pl.when(i >= OUT_SLOTS)
+    def _():
+        for c in stack_outs(i - OUT_SLOTS):
+            c.wait()
+
+    @pl.when(h == 0)
+    def _():
+        for q in range(TWO):
+            p_s[q] = times_right(e_p[g, q], block_diag(e_inv[g, q], R).T)
+            rts_s[q] = scale_rows(e_rt[g, q], e_n[g, q])
+        pt_s[:] = times_left(block_diag(e_inv[g, 2], R), jnp.concatenate([d_pt[g, 0], d_pt[g, 1]], 1))
+        r_s[0] = d_r[g] * (1.0 - MOMENTUM)
+        qpack = d_r[g] * d_n[g][:1]
+        r_s[1] = qpack * step
+        qrow_s[:] = qpack.T
+
+    @pl.when(h == 1)
+    def _():
+        for q in range(TWO):
+            p_s[q] = pltpu.roll(p_s[q], RD, 1)
+            r_s[q] = pltpu.roll(r_s[q], RD, 1)
+
+    half = pl.ds(h * RD, RD)
+    for q, x in enumerate((lambda m: x_g.at[i * 2 + m], lambda m: x_u.at[ins_slot, m])):
+        keep_update(p_s[q], e_rt[g, q, half], rts_s[q, half], R, x, lambda m: b_e.at[q, i * 2 + m],
+                    lambda m: out_e.at[slot, q, 0, m], lambda m: out_e.at[slot, q, 1, m],
+                    lambda m: outq_e.at[slot, q, m], step)
+    rcopies = lane_copies(r_s[0], R, range(TWO))
+    qcopies = lane_copies(r_s[1], R, range(TWO))
+    pt, qrows = pt_s[half], qrow_s[half]
+    for m in range(TWO):
+        rows = slice(R * m, R * m + R)
+        out = dot(jnp.concatenate([left_tiles(rcopies[m], R), left_tiles(qcopies[m], R)], 0), right_tiles(pt[rows], R))
+        out_d[slot, 1, m] = b_d[i * 2 + m] - out[:L]
+        out_d[slot, 0, m] = x_d[ins_slot, m] - out[L:]
+        outq_d[slot, m] = qrows[rows]
+    for c in stack_outs(i):
+        c.start()
+
+    @pl.when(i < 2 * NG - IN_SLOTS)
+    def _():
+        for c in stack_ins(i + IN_SLOTS):
+            c.start()
 
     @pl.when(i == 1)
     def _():
         for c in ins:
             c.wait()
-        keep_update(kv_p[:], kv_inv[:], kv_rt[:], kv_n[:], R, range(2),
-                    xs_kv.at.__getitem__, b_kv.at.__getitem__,
-                    xs_kv.at.__getitem__, mt_kv.at.__getitem__, qt_kv.at.__getitem__, step)
-        keep_update(qo_p[:], qo_inv[:], qo_rt[:], qo_n[:], RD, range(2),
-                    xs_qo.at.__getitem__, b_qo.at.__getitem__,
-                    xs_qo.at.__getitem__, mt_qo.at.__getitem__, qt_qo.at.__getitem__, LEARN_RATE)
+        for p0, inv, rt, n, rank, xs, b, mt, qt, size in (
+                (kv_p, kv_inv, kv_rt, kv_n, R, xs_kv, b_kv, mt_kv, qt_kv, step),
+                (qo_p, qo_inv, qo_rt, qo_n, RD, xs_qo, b_qo, mt_qo, qt_qo, LEARN_RATE)):
+            keep_update(times_right(p0[:], block_diag(inv[:], rank).T), rt[:], scale_rows(rt[:], n[:]), rank,
+                        xs.at.__getitem__, b.at.__getitem__,
+                        xs.at.__getitem__, mt.at.__getitem__, qt.at.__getitem__, size)
         for c in outs:
             c.start()
 
-    @pl.when(i == NG - 1)
+    @pl.when(i == 2 * NG - 1)
     def _():
         for c in outs:
             c.wait()
+        for k in range(OUT_SLOTS):
+            for c in stack_outs(i - k):
+                c.wait()
 
 
 def run_final(xs, packs):
     hbm = pl.BlockSpec(memory_space=pl.ANY)
     v = pltpu.VMEM
-
-    def spec(a):
-        return pl.BlockSpec((PACK,) + a.shape[1:], lambda i: (i, 0, 0))
 
     out = lambda *shape: jax.ShapeDtypeStruct(shape, F32)
     big = [out(R, H, H), out(R, H, H), out(R, R, H)]
@@ -658,12 +710,17 @@
     narrow = [out(H, H), out(H, H), out(R, H)]
     return pl.pallas_call(
         final_kernel,
-        grid=(NG,),
+        grid=(2 * NG,),
         out_shape=stacks + wide + narrow + narrow + wide,
-        in_specs=[spec(a) for a in xs[:3]] + [hbm] * 4 + [pl.BlockSpec(memory_space=v)] * len(packs),
-        out_specs=[spec(a) for a in stacks] + [hbm] * 12,
-        scratch_shapes=[v((2, H, H), F32), v((2, H, W), F32), v((2, H, H), F32), v((2, H, W), F32),
-                        v((2, R, H), F32), v((2, RD, W), F32),
+        in_specs=[hbm] * len(xs) + [pl.BlockSpec(memory_space=v)] * len(packs),
+        out_specs=[hbm] * len(stacks + wide + narrow + narrow + wide),
+        scratch_shapes=[v((IN_SLOTS, TWO, H, H), F32), v((IN_SLOTS, TWO, L, W), F32),
+                        pltpu.SemaphoreType.DMA((TWO, IN_SLOTS)), v((OUT_SLOTS, TWO, TWO, TWO, H, H), F32), v((OUT_SLOTS, TWO, TWO, R, H), F32),
+                        v((OUT_SLOTS, TWO, TWO, L, W), F32), v((OUT_SLOTS, 2, R, L), F32),
+                        pltpu.SemaphoreType.DMA((len(stacks), OUT_SLOTS)),
+                        v((TWO, H, L), F32), v((TWO, L, H), F32), v((TWO, L, L), F32), v((L, W), F32), v((L, L), F32),
+                        v((TWO, H, H), F32), v((TWO, H, W), F32), v((TWO, H, H), F32), v((TWO, H, W), F32),
+                        v((TWO, R, H), F32), v((TWO, RD, W), F32),
                         pltpu.SemaphoreType.DMA((4,)), pltpu.SemaphoreType.DMA((12,))],
         name="final_kernel",
         compiler_params=pltpu.CompilerParams(vmem_limit_bytes=FINAL_VMEM, dimension_semantics=("arbitrary",)),
@@ -685,8 +742,9 @@
         comm_in = []
         for i in (4, 5, 6, 0, 1, 2, 3):
             comm_in += [m[i], g[i], q[i]]
+        comm_in.append(x[4])
         packs = [pltpu.with_memory_space_constraint(a, pltpu.VMEM) for a in run_comm(comm_in)]
-        outs = run_final([x[i] for i in (4, 5, 6, 0, 1, 2, 3)], packs)
+        outs = run_final([x[i] for i in (5, 6, 0, 1, 2, 3)], packs)
         outs = list(outs[9:]) + list(outs[:9])
         for i in range(2, 21, 3):
             outs[i] = jnp.swapaxes(outs[i], -1, -2)

time: 114 us -> 108 us (0.947)
  Pallas kernels: 113 us -> 107 us
    pallas_call x1, Pallas kernels: 30.1 us -> 24.5 us  [run_final(): pl.pallas_call(final_kernel, grid=(2 * NG,), out_shape=stacks + wide + na...]
where the time goes in v3:
time: 108 us
  Pallas kernels  107 us (99%)
    pallas_call x1, Pallas kernels, run_comm(): pl.pallas_call(comm_kernel, out_shape=out_shape, in_specs=[pl.BlockSpec(m...  82.6 us
    pallas_call x1, Pallas kernels, run_final(): pl.pallas_call(final_kernel, grid=(2 * NG,), out_shape=stacks + wide + na...  24.5 us

profile of v3, /device:TPU:0, one launch (start us, length us, event | category | flops | bytes accessed | tf_op | source)
XLA Modules:
  0.0 108.0 jit_solution(12001063396370873185)
XLA Ops:
  0.7 82.6 %comm_kernel.1 = (f32[32,256,256]{2,1,0:T(8,128)S(1)}, f32[2,32,256,256]{3,2,1,0:T(8,128)S(1)}, f32[32,128,512]{2,1,0:T(8,128)S(1)}, f32[2,256,256]{2,1,0:T(8,12...) custom-call(f32[32,256,256]{2,1,0:T(8,128)} %gm.1, ...), custom_call_target="tpu_custom_call" | custom-call | tf_op jit(solution)/shard_map/comm_kernel/pallas_call | solution.py:530
  83.3 24.5 %final_kernel.1 = (f32[32,256,256]{2,1,0:T(8,128)}, f32[32,256,256]{2,1,0:T(8,128)}, f32[32,32,256]{2,1,0:T(8,128)}, f32[32,256,256]{2,1,0:T(8,128)}, f32[32,256...) custom-call(f32[32,256,256]{2,1,0:T(8,128)} %ux.1, ...), custom_call_target="tpu_custom_call" | custom-call | tf_op jit(solution)/shard_map/final_kernel/pallas_call | solution.py:711

commit v4 on v3

--- a/solution.py
+++ b/solution.py
@@ -23,8 +23,9 @@
 FINAL_VMEM = 22 << 20
 NORM_LAG = 4
 OUT_SLOTS = 3
-IN_SLOTS = 4
+IN_SLOTS = 5
 TWO = 2
+HR = R // 2
 SH = 72
 
 
@@ -85,9 +86,9 @@
     base = (lane // rank) * rank
     col = lane - base
     mats = list(grams)
-    for k0 in range(0, rank, 8):
-        cols = [[jnp.take_along_axis(a, base + (k0 + j), axis=1) for j in range(8)] for a in mats]
-        for j in range(8):
+    for k0 in range(0, rank, 16):
+        cols = [[jnp.take_along_axis(a, base + (k0 + j), axis=1) for j in range(16)] for a in mats]
+        for j in range(16):
             k = k0 + j
             below = row > k
             for i, a in enumerate(mats):
@@ -95,7 +96,7 @@
                 factor = jnp.where(below, ck * (1.0 / ck[k:k + 1]), 0.0)
                 pivot = jnp.where(col[:1] == k, 1.0, a[k:k + 1])
                 mats[i] = jnp.where(below & (col == k), 0.0, a) - factor * pivot
-                for l in range(j + 1, 8):
+                for l in range(j + 1, 16):
                     cl = cols[i][l]
                     cols[i][l] = cl - factor * cl[k:k + 1]
     out = []
@@ -160,7 +161,7 @@
                 kv_inv, kv_p, kv_rt, kv_n, qo_inv, qo_p, qo_rt, qo_n,
                 gs_e, gs_d, qs_e, qs_d, gs_kv, qs_kv, gs_qo, qs_qo,
                 z_e, z_d, z_kv, z_qo,
-                pown, prcv, down, drc1, dxs, dxr, sown, src1, sxs, sxr, stf, zown, zrcv,
+                pown, prcv, down, drc1, dxs, dxr, sown, src1, sxs, sxr, stf, zown, zrcv, zw, zt,
                 nown, nrcv, dnown, dnrcv,
                 kpo, kpr, kso, ksr, kxs, kxr, kst, kno, knr,
                 qpo, qpr, qso, qsr, qxs, qxr, qst, qno, qnr,
@@ -227,6 +228,10 @@
 
     def c_z(g):
         return remote(zown.at[lax.rem(g, 2)], zrcv.at[lax.rem(g, 3)], send.at[5, g], recv.at[5, g], ypeer)
+
+    def c_w(g):
+        s = lax.rem(g, 2)
+        return remote(zt.at[s, core], zt.at[s, core], send.at[7, g], recv.at[7, g], sib)
 
     def c_n(g):
         return remote(nown.at[g], nrcv.at[g], send.at[6, g], recv.at[6, g], ypeer)
@@ -354,8 +359,17 @@
         vt = jnp.concatenate([d_pt[g, 0], d_pt[g, 1]], 1)
         v = vt.T
         zown[s, pl.ds(0, L)] = row_factor(lambda m: pieces_of(z_d.at[m]), PACK, v, R)
-        zown[s, pl.ds(L, R)] = gram(split3(vt), split3(v), R)
+        w = gram(split3(vt), split3(v), R)
+        zw[0] = w[:HR]
+        zw[1] = w[HR:]
+        zown[s, pl.ds(L, HR)] = zw[core]
         c_z(g).start()
+
+    def stage3w(g):
+        s = lax.rem(g, 2)
+        c_z(g).wait()
+        zt[s, core] = zown[s, pl.ds(L, HR)] + zrcv[lax.rem(g, 3), pl.ds(L, HR)]
+        c_w(g).start()
 
     def stage2_dense():
         kc[0]().wait()
@@ -406,17 +420,17 @@
         s = lax.rem(g, 2)
         for q in range(2):
             c_s3(g, q).wait()
-        c_z(g).wait()
-        z = zown[s] + zrcv[lax.rem(g, 3)]
+        c_w(g).wait()
+        z = zown[s, pl.ds(0, L)] + zrcv[lax.rem(g, 3), pl.ds(0, L)]
         ws = [rows_to_gram([stf[s, h, q, pl.ds(RD, 8)] for h in range(2)], R) for q in range(2)]
-        inv = inverse_factors(ws + [z[L:]], R)
+        inv = inverse_factors(ws + [jnp.concatenate([zt[s, 0], zt[s, 1]], 0)], R)
         for i in range(3):
             e_inv[g, i] = inv[i]
         for q in range(2):
             apply_keep(e_rt.at[g, q], nown.at[g, q], inv[q], stf.at[s, :, q], R)
         c_n(g).start()
         bd = block_diag(inv[2], R)
-        r = times_right(z[:L], bd.T)
+        r = times_right(z, bd.T)
         d_r[g] = r
         dnown[g] = sq_lanes(r)
         for c in c_nd(g):
@@ -488,6 +502,7 @@
         within(1, lambda g: stage3a(g, 0))
         within(2, stage3b)
         only(1, stage3b_dense)
+        within(2, stage3w)
         within(1, stage2c_down)
         within(1, lambda g: stage3a(g, 1))
         only(0, stage3a_dense)
@@ -523,10 +538,10 @@
         v((TWO, TWO, L, H), F32), v((TWO, L, H), F32), v((TWO, L, H), F32), v((3, L, H), F32),
         v((TWO, TWO, TWO, SH, H), F32), v((TWO, TWO, SH, H), F32), v((TWO, TWO, SH, H), F32), v((3, 2, SH, H), F32),
         v((TWO, TWO, TWO, SH, H), F32),
-        v((TWO, L + R, L), F32), v((3, L + R, L), F32),
+        v((TWO, L + HR, L), F32), v((3, L + HR, L), F32), v((TWO, HR, L), F32), v((TWO, TWO, HR, L), F32),
         v((NG, 2, 8, L), F32), v((NG, 2, 8, L), F32), v((NG, 8, L), F32), v((NG, 3, 8, L), F32),
     ] + pack_bufs(L, H) + pack_bufs(H, W) + [
-        dma((2, 9)), dma((13,)), dma((7, NG)), dma((7, NG)), dma((3, 2, NG)), dma((3, 2, NG)), dma((2, 5)), dma((2, 5)), dma((3, NG)), dma((3, NG))]
+        dma((2, 9)), dma((13,)), dma((8, NG)), dma((8, NG)), dma((3, 2, NG)), dma((3, 2, NG)), dma((2, 5)), dma((2, 5)), dma((3, NG)), dma((3, NG))]
     return pl.pallas_call(
         comm_kernel,
         out_shape=out_shape,

time: 108 us -> 107 us (level)
  no operation moved by 1% of the time
where the time goes in v4:
time: 107 us
  Pallas kernels  106 us (99%)
    pallas_call x1, Pallas kernels, run_comm(): pl.pallas_call(comm_kernel, out_shape=out_shape, in_specs=[pl.BlockSpec(m...  82.2 us
    pallas_call x1, Pallas kernels, run_final(): pl.pallas_call(final_kernel, grid=(2 * NG,), out_shape=stacks + wide + na...  24.2 us

profile of v4, /device:TPU:0, one launch (start us, length us, event | category | flops | bytes accessed | tf_op | source)
XLA Modules:
  0.0 107.2 jit_solution(5624529232033095696)
XLA Ops:
  0.7 82.2 %comm_kernel.1 = (f32[32,256,256]{2,1,0:T(8,128)S(1)}, f32[2,32,256,256]{3,2,1,0:T(8,128)S(1)}, f32[32,128,512]{2,1,0:T(8,128)S(1)}, f32[2,256,256]{2,1,0:T(8,12...) custom-call(f32[32,256,256]{2,1,0:T(8,128)} %gm.1, ...), custom_call_target="tpu_custom_call" | custom-call | tf_op jit(solution)/shard_map/comm_kernel/pallas_call | solution.py:545
  82.9 24.2 %final_kernel.1 = (f32[32,256,256]{2,1,0:T(8,128)}, f32[32,256,256]{2,1,0:T(8,128)}, f32[32,32,256]{2,1,0:T(8,128)}, f32[32,256,256]{2,1,0:T(8,128)}, f32[32,256...) custom-call(f32[32,256,256]{2,1,0:T(8,128)} %ux.1, ...), custom_call_target="tpu_custom_call" | custom-call | tf_op jit(solution)/shard_map/final_kernel/pallas_call | solution.py:726
